TPU v7x, 128 devices: a whole 4x4x4 slice. The times are simulated.
128 devices in a mesh: data: 1, model: 2 (over core), time: 64 (over z, y, x).
Axes of the slice: x: 4, y: 4, z: 4, core: 2. Of those that a mesh axis runs over, the one named last changes fastest.
Arguments:
- x_init: float32 [4, 4096, 16], P('data')
- w_up: bfloat16 [16, 1152], P(None, 'model')
- w_down: bfloat16 [1152, 16], P('model')
- mod_scale: bfloat16 [384, 1152], P('time', 'model')
- mod_shift: bfloat16 [384, 1152], P('time', 'model')
- step_size: float32 [384], P('time')
Outputs:
- output: float32 [384, 4, 4096, 16], P('time', 'data')
All inputs are finite; a program needn't handle non-finite values.
Results may differ from a plain program's by a relative error of at most 0.001.
Values are sent between devices in bfloat16 or wider.
A program may use at most 1 GiB of HBM per device.

v0:
```python
import jax
import jax.numpy as jnp
from jax import lax
from jax.sharding import PartitionSpec as P

SWEEPS = 4


def local_drift(latents, w_up, w_down, scale_f, shift_f):
    pre_act = jnp.einsum('tbnc,cd->tbnd', latents.astype(jnp.bfloat16), w_up, preferred_element_type=jnp.float32)
    hidden = jax.nn.gelu(pre_act * scale_f[:, None, None, :] + shift_f[:, None, None, :], approximate=True)
    return jnp.einsum('tbnd,dc->tbnc', hidden.astype(jnp.bfloat16), w_down, preferred_element_type=jnp.float32)


def solution(mesh):
    time_devs = mesh.shape['time']

    def device_body(x_init, w_up, w_down, mod_scale, mod_shift, step_size):
        scale_f = 1.0 + mod_scale.astype(jnp.float32)
        shift_f = mod_shift.astype(jnp.float32)
        step_col = step_size[:, None, None, None]
        latents = jnp.broadcast_to(x_init[None], (mod_scale.shape[0],) + x_init.shape)
        for sweep_idx in range(SWEEPS):
            part_drift = local_drift(latents, w_up, w_down, scale_f, shift_f)
            drifts = step_col * lax.psum(part_drift, 'model')
            running = jnp.cumsum(drifts, axis=0)
            dev_total = running[-1]
            scan_acc = dev_total
            shift_len = 1
            while shift_len < time_devs:
                perm_pairs = [(source_idx, source_idx + shift_len) for source_idx in range(time_devs - shift_len)]
                scan_acc = scan_acc + lax.ppermute(scan_acc, 'time', perm_pairs)
                shift_len = shift_len * 2
            offset = scan_acc - dev_total
            latents = (x_init + offset)[None] + (running - drifts)
        return latents

    return jax.shard_map(device_body, mesh=mesh, in_specs=(P('data', None, None), P(None, 'model'), P('model', None), P('time', 'model'), P('time', 'model'), P('time')), out_specs=P('time', 'data', None, None), check_vma=False)
```

profile of v0, /device:TPU:1, one launch (start us, length us, event | category | flops | bytes accessed | tf_op | source)
XLA Modules:
  0.0 1327.1 jit_solution(2303396048314334010)
XLA Ops:
  9.3 100.4 %fusion.38 = f32[6,4,4096,16]{2,3,1,0:T(8,128)} fusion(f32[6,576]{1,0:T(8,128)S(1)} %convert_element_type.33, f32[6,576]{1,0:T(8,128)S(1)} %convert_add_fusion, bf16[4,4096,16]{1,2,0:T(8,128)(2,1)S(1)} %convert_element_type.31, bf16[576,16]{0,1:T(8,128)(2,1)} %param.8, bf16[16,576]{1,0:T(8,128)(2,1)S(1)} %copy-done), kind=kOutput, calls=%fused_computation.39 | convolution fusion | flops 4246732800 | bytes 6880256 | tf_op jit(solution)/shard_map/tbnd,dc->tbnc/dot_general | solution.py:12
  109.7 39.1 %all-reduce.5.cloned.1.call-done = f32[6,4,4096,16]{2,3,1,0:T(8,128)} async-done(((f32[6,4,4096,16]{2,3,1,0:T(8,128)}), f32[6,4,4096,16]{2,3,1,0:T(8,128)}) %all-reduce.5.cloned.1.call-update) | async-done | bytes 6291472 | tf_op jit(solution)/shard_map/psum | solution.py:25
  156.0 22.2 %collective-permute-done = f32[4,4096,16]{1,2,0:T(8,128)S(1)} collective-permute-done((f32[4,4096,16]{1,2,0:T(8,128)S(1)}, f32[4,4096,16]{1,2,0:T(8,128)S(1)}, u32[]{:S(2)}, u32[]{:S(2)}) %collective-permute-start) | collective-permute-done | bytes 1048608 | tf_op jit(solution)/shard_map/ppermute | solution.py:32
  184.2 21.3 %collective-permute-done.1 = f32[4,4096,16]{1,2,0:T(8,128)S(1)} collective-permute-done((f32[4,4096,16]{1,2,0:T(8,128)S(1)}, f32[4,4096,16]{1,2,0:T(8,128)S(1)}, u32[]{:S(2)}, u32[]{:S(2)}) %collective-permute-start.1) | collective-permute-done | bytes 1048608 | tf_op jit(solution)/shard_map/ppermute | solution.py:32
  212.6 19.8 %collective-permute-done.2 = f32[4,4096,16]{1,2,0:T(8,128)S(1)} collective-permute-done((f32[4,4096,16]{1,2,0:T(8,128)S(1)}, f32[4,4096,16]{1,2,0:T(8,128)S(1)}, u32[]{:S(2)}, u32[]{:S(2)}) %collective-permute-start.2) | collective-permute-done | bytes 1048608 | tf_op jit(solution)/shard_map/ppermute | solution.py:32
  306.0 99.7 %fusion.125 = bf16[6,4,4096,576]{2,3,1,0:T(8,128)(2,1)} fusion(f32[6,576]{1,0:T(8,128)S(1)} %convert_element_type.33, f32[6,576]{1,0:T(8,128)S(1)} %convert_add_fusion, f32[6,4,4096,16]{2,3,1,0:T(8,128)} %copy-done.6, f32[6,4,4096,16]{2,3,1,0:T(8,128)} %all-reduce.5.cloned.1.call-done, f32[4,4096,16]{1,2,0:T(8,128)S(1)} %subtract_add_fusion.4, ...), kind=kOutput, calls=%fused_computation.19.clone.clone | convolution fusion | flops 2441084928 | bytes 126923800 | tf_op jit(solution)/shard_map/tbnc,cd->tbnd/dot_general | solution.py:10
  405.7 39.3 %fusion.36 = f32[6,4,4096,16]{2,3,1,0:T(8,128)} fusion(bf16[576,16]{0,1:T(8,128)(2,1)S(1)} %copy-done.8, bf16[6,4,4096,576]{2,3,1,0:T(8,128)(2,1)} %fusion.125), kind=kOutput, calls=%fused_computation.38 | convolution fusion | flops 1811939328 | bytes 119556096 | tf_op jit(solution)/shard_map/tbnd,dc->tbnc/dot_general | solution.py:12
  445.1 40.3 %all-reduce.7.cloned.1.call-done = f32[6,4,4096,16]{2,3,1,0:T(8,128)} async-done(((f32[6,4,4096,16]{2,3,1,0:T(8,128)}), f32[6,4,4096,16]{2,3,1,0:T(8,128)}) %all-reduce.7.cloned.1.call-update) | async-done | bytes 6291472 | tf_op jit(solution)/shard_map/psum | solution.py:25
  492.5 22.2 %collective-permute-done.6 = f32[4,4096,16]{1,2,0:T(8,128)S(1)} collective-permute-done((f32[4,4096,16]{1,2,0:T(8,128)S(1)}, f32[4,4096,16]{1,2,0:T(8,128)S(1)}, u32[]{:S(2)}, u32[]{:S(2)}) %collective-permute-start.6) | collective-permute-done | bytes 1048608 | tf_op jit(solution)/shard_map/ppermute | solution.py:32
  520.7 21.3 %collective-permute-done.7 = f32[4,4096,16]{1,2,0:T(8,128)S(1)} collective-permute-done((f32[4,4096,16]{1,2,0:T(8,128)S(1)}, f32[4,4096,16]{1,2,0:T(8,128)S(1)}, u32[]{:S(2)}, u32[]{:S(2)}) %collective-permute-start.7) | collective-permute-done | bytes 1048608 | tf_op jit(solution)/shard_map/ppermute | solution.py:32
  549.1 19.8 %collective-permute-done.8 = f32[4,4096,16]{1,2,0:T(8,128)S(1)} collective-permute-done((f32[4,4096,16]{1,2,0:T(8,128)S(1)}, f32[4,4096,16]{1,2,0:T(8,128)S(1)}, u32[]{:S(2)}, u32[]{:S(2)}) %collective-permute-start.8) | collective-permute-done | bytes 1048608 | tf_op jit(solution)/shard_map/ppermute | solution.py:32
  642.5 99.7 %fusion.122 = bf16[6,4,4096,576]{2,3,1,0:T(8,128)(2,1)} fusion(f32[6,576]{1,0:T(8,128)S(1)} %convert_element_type.33, f32[6,576]{1,0:T(8,128)S(1)} %convert_add_fusion, f32[6,4,4096,16]{2,3,1,0:T(8,128)} %copy-done.7, f32[6,4,4096,16]{2,3,1,0:T(8,128)} %all-reduce.7.cloned.1.call-done, f32[4,4096,16]{1,2,0:T(8,128)S(1)} %subtract_add_fusion.3, ...), kind=kOutput, calls=%fused_computation.27.clone.clone | convolution fusion | flops 2441084928 | bytes 126923800 | tf_op jit(solution)/shard_map/tbnc,cd->tbnd/dot_general | solution.py:10
  742.2 39.5 %fusion.34 = f32[6,4,4096,16]{2,3,1,0:T(8,128)} fusion(bf16[576,16]{0,1:T(8,128)(2,1)S(1)} %copy-done.9, bf16[6,4,4096,576]{2,3,1,0:T(8,128)(2,1)} %fusion.122), kind=kOutput, calls=%fused_computation.37 | convolution fusion | flops 1811939328 | bytes 119556096 | tf_op jit(solution)/shard_map/tbnd,dc->tbnc/dot_general | solution.py:12
  781.8 40.3 %all-reduce.9.cloned.1.call-done = f32[6,4,4096,16]{2,3,1,0:T(8,128)} async-done(((f32[6,4,4096,16]{2,3,1,0:T(8,128)}), f32[6,4,4096,16]{2,3,1,0:T(8,128)}) %all-reduce.9.cloned.1.call-update) | async-done | bytes 6291472 | tf_op jit(solution)/shard_map/psum | solution.py:25
  829.2 22.2 %collective-permute-done.12 = f32[4,4096,16]{1,2,0:T(8,128)S(1)} collective-permute-done((f32[4,4096,16]{1,2,0:T(8,128)S(1)}, f32[4,4096,16]{1,2,0:T(8,128)S(1)}, u32[]{:S(2)}, u32[]{:S(2)}) %collective-permute-start.12) | collective-permute-done | bytes 1048608 | tf_op jit(solution)/shard_map/ppermute | solution.py:32
  857.4 21.3 %collective-permute-done.13 = f32[4,4096,16]{1,2,0:T(8,128)S(1)} collective-permute-done((f32[4,4096,16]{1,2,0:T(8,128)S(1)}, f32[4,4096,16]{1,2,0:T(8,128)S(1)}, u32[]{:S(2)}, u32[]{:S(2)}) %collective-permute-start.13) | collective-permute-done | bytes 1048608 | tf_op jit(solution)/shard_map/ppermute | solution.py:32
  885.9 19.8 %collective-permute-done.14 = f32[4,4096,16]{1,2,0:T(8,128)S(1)} collective-permute-done((f32[4,4096,16]{1,2,0:T(8,128)S(1)}, f32[4,4096,16]{1,2,0:T(8,128)S(1)}, u32[]{:S(2)}, u32[]{:S(2)}) %collective-permute-start.14) | collective-permute-done | bytes 1048608 | tf_op jit(solution)/shard_map/ppermute | solution.py:32
  911.5 18.9 %collective-permute-done.15 = f32[4,4096,16]{1,2,0:T(8,128)S(1)} collective-permute-done((f32[4,4096,16]{1,2,0:T(8,128)S(1)}, f32[4,4096,16]{1,2,0:T(8,128)S(1)}, u32[]{:S(2)}, u32[]{:S(2)}) %collective-permute-start.15) | collective-permute-done | bytes 1048608 | tf_op jit(solution)/shard_map/ppermute | solution.py:32
  979.3 99.7 %fusion.119 = bf16[6,4,4096,576]{2,3,1,0:T(8,128)(2,1)} fusion(f32[6,576]{1,0:T(8,128)S(1)} %convert_element_type.33, f32[6,576]{1,0:T(8,128)S(1)} %convert_add_fusion, f32[6,4,4096,16]{2,3,1,0:T(8,128)} %copy-done.5, f32[6,4,4096,16]{2,3,1,0:T(8,128)} %all-reduce.9.cloned.1.call-done, f32[4,4096,16]{1,2,0:T(8,128)S(1)} %subtract_add_fusion.2, ...), kind=kOutput, calls=%fused_computation.35.clone.clone.1 | convolution fusion | flops 2441084928 | bytes 126923800 | tf_op jit(solution)/shard_map/tbnc,cd->tbnd/dot_general | solution.py:10
  1079.0 39.3 %fusion.32 = f32[6,4,4096,16]{2,3,1,0:T(8,128)} fusion(bf16[576,16]{0,1:T(8,128)(2,1)S(1)} %copy-done.10, bf16[6,4,4096,576]{2,3,1,0:T(8,128)(2,1)} %fusion.119), kind=kOutput, calls=%fused_computation.36 | convolution fusion | flops 1811939328 | bytes 119556096 | tf_op jit(solution)/shard_map/tbnd,dc->tbnc/dot_general | solution.py:12
  1118.3 40.3 %all-reduce.11.cloned.1.call-done = f32[6,4,4096,16]{2,3,1,0:T(8,128)} async-done(((f32[6,4,4096,16]{2,3,1,0:T(8,128)}), f32[6,4,4096,16]{2,3,1,0:T(8,128)}) %all-reduce.11.cloned.1.call-update) | async-done | bytes 6291472 | tf_op jit(solution)/shard_map/psum | solution.py:25
  1165.8 22.2 %collective-permute-done.18 = f32[4,4096,16]{1,2,0:T(8,128)S(1)} collective-permute-done((f32[4,4096,16]{1,2,0:T(8,128)S(1)}, f32[4,4096,16]{1,2,0:T(8,128)S(1)}, u32[]{:S(2)}, u32[]{:S(2)}) %collective-permute-start.18) | collective-permute-done | bytes 1048608 | tf_op jit(solution)/shard_map/ppermute | solution.py:32
  1194.0 21.3 %collective-permute-done.19 = f32[4,4096,16]{1,2,0:T(8,128)S(1)} collective-permute-done((f32[4,4096,16]{1,2,0:T(8,128)S(1)}, f32[4,4096,16]{1,2,0:T(8,128)S(1)}, u32[]{:S(2)}, u32[]{:S(2)}) %collective-permute-start.19) | collective-permute-done | bytes 1048608 | tf_op jit(solution)/shard_map/ppermute | solution.py:32
  1222.4 19.8 %collective-permute-done.20 = f32[4,4096,16]{1,2,0:T(8,128)S(1)} collective-permute-done((f32[4,4096,16]{1,2,0:T(8,128)S(1)}, f32[4,4096,16]{1,2,0:T(8,128)S(1)}, u32[]{:S(2)}, u32[]{:S(2)}) %collective-permute-start.20) | collective-permute-done | bytes 1048608 | tf_op jit(solution)/shard_map/ppermute | solution.py:32
  (108 shorter events, 363.8 us)
Async XLA Ops:
  6.5 142.3 %all-reduce.5.cloned.1.call-start = ((), (), s32[]{:S(2)}) async-start(), calls=%async_computation | async-start | bytes 12582912 | tf_op jit(solution)/shard_map/psum | solution.py:25
  109.6 375.7 %all-reduce.7.cloned.1.call-start = ((), (), s32[]{:S(2)}) async-start(), calls=%async_computation.1 | async-start | bytes 12582912 | tf_op jit(solution)/shard_map/psum | solution.py:25
  152.7 25.5 %collective-permute-start = (f32[4,4096,16]{1,2,0:T(8,128)S(1)}, f32[4,4096,16]{1,2,0:T(8,128)S(1)}, u32[]{:S(2)}, u32[]{:S(2)}) collective-permute-start(f32[4,4096,16]{1,2,0:T(8,128)S(1)} %slice_bitcast_fusion.3), channel_id=1, source_target_pairs={{0,1},{1,2},{2,3},{3,4},{4,5},{5,6},{6,7},{7,8},{8,9},{9,10},{10,1... | collective-permute-start | bytes 3145736 | tf_op jit(solution)/shard_map/ppermute | solution.py:32
  178.3 27.2 %collective-permute-start.1 = (f32[4,4096,16]{1,2,0:T(8,128)S(1)}, f32[4,4096,16]{1,2,0:T(8,128)S(1)}, u32[]{:S(2)}, u32[]{:S(2)}) collective-permute-start(f32[4,4096,16]{1,2,0:T(8,128)S(1)} %fusion.102), channel_id=1, source_target_pairs={{0,2},{1,3},{2,4},{3,5},{4,6},{5,7},{6,8},{7,9},{8,10},{9,11},{10,... | collective-permute-start | bytes 3145736 | tf_op jit(solution)/shard_map/ppermute | solution.py:32
  205.6 26.7 %collective-permute-start.2 = (f32[4,4096,16]{1,2,0:T(8,128)S(1)}, f32[4,4096,16]{1,2,0:T(8,128)S(1)}, u32[]{:S(2)}, u32[]{:S(2)}) collective-permute-start(f32[4,4096,16]{1,2,0:T(8,128)S(1)} %add.187), channel_id=1, source_target_pairs={{0,4},{1,5},{2,6},{3,7},{4,8},{5,9},{6,10},{7,11},{8,12},{9,13},{1... | collective-permute-start | bytes 3145736 | tf_op jit(solution)/shard_map/ppermute | solution.py:32
  232.5 24.6 %collective-permute-start.3 = (f32[4,4096,16]{1,2,0:T(8,128)S(1)}, f32[4,4096,16]{1,2,0:T(8,128)S(1)}, u32[]{:S(2)}, u32[]{:S(2)}) collective-permute-start(f32[4,4096,16]{1,2,0:T(8,128)S(1)} %add.188), channel_id=1, source_target_pairs={{0,8},{1,9},{2,10},{3,11},{4,12},{5,13},{6,14},{7,15},{8,16},{9,17... | collective-permute-start | bytes 3145736 | tf_op jit(solution)/shard_map/ppermute | solution.py:32
  257.2 26.7 %collective-permute-start.4 = (f32[4,4096,16]{1,2,0:T(8,128)S(1)}, f32[4,4096,16]{1,2,0:T(8,128)S(1)}, u32[]{:S(2)}, u32[]{:S(2)}) collective-permute-start(f32[4,4096,16]{1,2,0:T(8,128)S(1)} %add.189), channel_id=1, source_target_pairs={{0,16},{1,17},{2,18},{3,19},{4,20},{5,21},{6,22},{7,23},{8,24},{9,... | collective-permute-start | bytes 3145736 | tf_op jit(solution)/shard_map/ppermute | solution.py:32
  445.0 377.1 %all-reduce.9.cloned.1.call-start = ((), (), s32[]{:S(2)}) async-start(), calls=%async_computation.2 | async-start | bytes 12582912 | tf_op jit(solution)/shard_map/psum | solution.py:25
  489.2 25.5 %collective-permute-start.6 = (f32[4,4096,16]{1,2,0:T(8,128)S(1)}, f32[4,4096,16]{1,2,0:T(8,128)S(1)}, u32[]{:S(2)}, u32[]{:S(2)}) collective-permute-start(f32[4,4096,16]{1,2,0:T(8,128)S(1)} %slice_bitcast_fusion.2), channel_id=1, source_target_pairs={{0,1},{1,2},{2,3},{3,4},{4,5},{5,6},{6,7},{7,8},{8,9},{9,10},{10,1... | collective-permute-start | bytes 3145736 | tf_op jit(solution)/shard_map/ppermute | solution.py:32
  514.8 27.2 %collective-permute-start.7 = (f32[4,4096,16]{1,2,0:T(8,128)S(1)}, f32[4,4096,16]{1,2,0:T(8,128)S(1)}, u32[]{:S(2)}, u32[]{:S(2)}) collective-permute-start(f32[4,4096,16]{1,2,0:T(8,128)S(1)} %fusion.103), channel_id=1, source_target_pairs={{0,2},{1,3},{2,4},{3,5},{4,6},{5,7},{6,8},{7,9},{8,10},{9,11},{10,... | collective-permute-start | bytes 3145736 | tf_op jit(solution)/shard_map/ppermute | solution.py:32
  542.1 26.7 %collective-permute-start.8 = (f32[4,4096,16]{1,2,0:T(8,128)S(1)}, f32[4,4096,16]{1,2,0:T(8,128)S(1)}, u32[]{:S(2)}, u32[]{:S(2)}) collective-permute-start(f32[4,4096,16]{1,2,0:T(8,128)S(1)} %add.199), channel_id=1, source_target_pairs={{0,4},{1,5},{2,6},{3,7},{4,8},{5,9},{6,10},{7,11},{8,12},{9,13},{1... | collective-permute-start | bytes 3145736 | tf_op jit(solution)/shard_map/ppermute | solution.py:32
  569.0 24.6 %collective-permute-start.9 = (f32[4,4096,16]{1,2,0:T(8,128)S(1)}, f32[4,4096,16]{1,2,0:T(8,128)S(1)}, u32[]{:S(2)}, u32[]{:S(2)}) collective-permute-start(f32[4,4096,16]{1,2,0:T(8,128)S(1)} %add.200), channel_id=1, source_target_pairs={{0,8},{1,9},{2,10},{3,11},{4,12},{5,13},{6,14},{7,15},{8,16},{9,17... | collective-permute-start | bytes 3145736 | tf_op jit(solution)/shard_map/ppermute | solution.py:32
  593.7 26.7 %collective-permute-start.10 = (f32[4,4096,16]{1,2,0:T(8,128)S(1)}, f32[4,4096,16]{1,2,0:T(8,128)S(1)}, u32[]{:S(2)}, u32[]{:S(2)}) collective-permute-start(f32[4,4096,16]{1,2,0:T(8,128)S(1)} %add.201), channel_id=1, source_target_pairs={{0,16},{1,17},{2,18},{3,19},{4,20},{5,21},{6,22},{7,23},{8,24},{9,... | collective-permute-start | bytes 3145736 | tf_op jit(solution)/shard_map/ppermute | solution.py:32
  781.8 376.9 %all-reduce.11.cloned.1.call-start = ((), (), s32[]{:S(2)}) async-start(), calls=%async_computation.3 | async-start | bytes 12582912 | tf_op jit(solution)/shard_map/psum | solution.py:25
  826.0 25.5 %collective-permute-start.12 = (f32[4,4096,16]{1,2,0:T(8,128)S(1)}, f32[4,4096,16]{1,2,0:T(8,128)S(1)}, u32[]{:S(2)}, u32[]{:S(2)}) collective-permute-start(f32[4,4096,16]{1,2,0:T(8,128)S(1)} %slice_bitcast_fusion.1), channel_id=1, source_target_pairs={{0,1},{1,2},{2,3},{3,4},{4,5},{5,6},{6,7},{7,8},{8,9},{9,10},{10,1... | collective-permute-start | bytes 3145736 | tf_op jit(solution)/shard_map/ppermute | solution.py:32
  851.6 27.2 %collective-permute-start.13 = (f32[4,4096,16]{1,2,0:T(8,128)S(1)}, f32[4,4096,16]{1,2,0:T(8,128)S(1)}, u32[]{:S(2)}, u32[]{:S(2)}) collective-permute-start(f32[4,4096,16]{1,2,0:T(8,128)S(1)} %fusion.104), channel_id=1, source_target_pairs={{0,2},{1,3},{2,4},{3,5},{4,6},{5,7},{6,8},{7,9},{8,10},{9,11},{10,... | collective-permute-start | bytes 3145736 | tf_op jit(solution)/shard_map/ppermute | solution.py:32
  878.9 26.7 %collective-permute-start.14 = (f32[4,4096,16]{1,2,0:T(8,128)S(1)}, f32[4,4096,16]{1,2,0:T(8,128)S(1)}, u32[]{:S(2)}, u32[]{:S(2)}) collective-permute-start(f32[4,4096,16]{1,2,0:T(8,128)S(1)} %add.211), channel_id=1, source_target_pairs={{0,4},{1,5},{2,6},{3,7},{4,8},{5,9},{6,10},{7,11},{8,12},{9,13},{1... | collective-permute-start | bytes 3145736 | tf_op jit(solution)/shard_map/ppermute | solution.py:32
  905.7 24.6 %collective-permute-start.15 = (f32[4,4096,16]{1,2,0:T(8,128)S(1)}, f32[4,4096,16]{1,2,0:T(8,128)S(1)}, u32[]{:S(2)}, u32[]{:S(2)}) collective-permute-start(f32[4,4096,16]{1,2,0:T(8,128)S(1)} %add.212), channel_id=1, source_target_pairs={{0,8},{1,9},{2,10},{3,11},{4,12},{5,13},{6,14},{7,15},{8,16},{9,17... | collective-permute-start | bytes 3145736 | tf_op jit(solution)/shard_map/ppermute | solution.py:32
  930.5 26.7 %collective-permute-start.16 = (f32[4,4096,16]{1,2,0:T(8,128)S(1)}, f32[4,4096,16]{1,2,0:T(8,128)S(1)}, u32[]{:S(2)}, u32[]{:S(2)}) collective-permute-start(f32[4,4096,16]{1,2,0:T(8,128)S(1)} %add.213), channel_id=1, source_target_pairs={{0,16},{1,17},{2,18},{3,19},{4,20},{5,21},{6,22},{7,23},{8,24},{9,... | collective-permute-start | bytes 3145736 | tf_op jit(solution)/shard_map/ppermute | solution.py:32
  1162.5 25.5 %collective-permute-start.18 = (f32[4,4096,16]{1,2,0:T(8,128)S(1)}, f32[4,4096,16]{1,2,0:T(8,128)S(1)}, u32[]{:S(2)}, u32[]{:S(2)}) collective-permute-start(f32[4,4096,16]{1,2,0:T(8,128)S(1)} %slice_bitcast_fusion), channel_id=1, source_target_pairs={{0,1},{1,2},{2,3},{3,4},{4,5},{5,6},{6,7},{7,8},{8,9},{9,10},{10,1... | collective-permute-start | bytes 3145736 | tf_op jit(solution)/shard_map/ppermute | solution.py:32
  1188.1 27.2 %collective-permute-start.19 = (f32[4,4096,16]{1,2,0:T(8,128)S(1)}, f32[4,4096,16]{1,2,0:T(8,128)S(1)}, u32[]{:S(2)}, u32[]{:S(2)}) collective-permute-start(f32[4,4096,16]{1,2,0:T(8,128)S(1)} %fusion.105), channel_id=1, source_target_pairs={{0,2},{1,3},{2,4},{3,5},{4,6},{5,7},{6,8},{7,9},{8,10},{9,11},{10,... | collective-permute-start | bytes 3145736 | tf_op jit(solution)/shard_map/ppermute | solution.py:32
  1215.4 26.7 %collective-permute-start.20 = (f32[4,4096,16]{1,2,0:T(8,128)S(1)}, f32[4,4096,16]{1,2,0:T(8,128)S(1)}, u32[]{:S(2)}, u32[]{:S(2)}) collective-permute-start(f32[4,4096,16]{1,2,0:T(8,128)S(1)} %add.223), channel_id=1, source_target_pairs={{0,4},{1,5},{2,6},{3,7},{4,8},{5,9},{6,10},{7,11},{8,12},{9,13},{1... | collective-permute-start | bytes 3145736 | tf_op jit(solution)/shard_map/ppermute | solution.py:32
  1242.3 24.9 %collective-permute-start.21 = (f32[4,4096,16]{1,2,0:T(8,128)S(1)}, f32[4,4096,16]{1,2,0:T(8,128)S(1)}, u32[]{:S(2)}, u32[]{:S(2)}) collective-permute-start(f32[4,4096,16]{1,2,0:T(8,128)S(1)} %add.224), channel_id=1, source_target_pairs={{0,8},{1,9},{2,10},{3,11},{4,12},{5,13},{6,14},{7,15},{8,16},{9,17... | collective-permute-start | bytes 3145736 | tf_op jit(solution)/shard_map/ppermute | solution.py:32
  1267.3 26.9 %collective-permute-start.22 = (f32[4,4096,16]{1,2,0:T(8,128)S(1)}, f32[4,4096,16]{1,2,0:T(8,128)S(1)}, u32[]{:S(2)}, u32[]{:S(2)}) collective-permute-start(f32[4,4096,16]{1,2,0:T(8,128)S(1)} %add.225), channel_id=1, source_target_pairs={{0,16},{1,17},{2,18},{3,19},{4,20},{5,21},{6,22},{7,23},{8,24},{9,... | collective-permute-start | bytes 3145736 | tf_op jit(solution)/shard_map/ppermute | solution.py:32
  (18 other events, 1520.1 us)
Sparse Core Ops, SparseCore 0:
  109.8 39.0 all-reduce.4
  445.1 40.1 all-reduce.6
  781.9 40.1 all-reduce.8
  1118.4 40.1 all-reduce.10
where the time goes:
time: 1340 us; the launch traced here: 1330 us
  waiting for transfers between devices  619 us (46%)
  matrix products  517 us (39%)
  starting transfers between devices  151 us (11%)
  other arithmetic  25.4 us (2%)
  between operations  13.8 us (1%)
    ppermute x24, waiting for transfers between devices, device_body(): scan_acc = scan_acc + lax.ppermute(scan_acc, 'time', perm_pairs)  459 us
    dot_general x3, matrix products, local_drift(): jnp.einsum('tbnc,cd->tbnd', latents.astype(jnp.bfloat16), w_up, preferred...  299 us
    dot_general x4, matrix products, local_drift(): jnp.einsum('tbnd,dc->tbnc', hidden.astype(jnp.bfloat16), w_down, preferre...  218 us
    psum x4, waiting for transfers between devices, device_body(): drifts = step_col * lax.psum(part_drift, 'model')  160 us
    ppermute x24, starting transfers between devices, device_body(): scan_acc = scan_acc + lax.ppermute(scan_acc, 'time', perm_pairs)  151 us
  transfers between devices with their start and end apart: 28, of which 28 were waited for; matrix products, arithmetic and copies ran while one was open for 0% of the time, Pallas kernels for 0%

commit v1 on v0

v1 whole, which is shorter than its diff:
```python
import functools
import math

import jax
import jax.numpy as jnp
from jax import lax
from jax.experimental import pallas as pl
from jax.experimental.pallas import tpu as pltpu
from jax.sharding import PartitionSpec as P

MESH = pl.DeviceIdType.MESH
BF = jnp.bfloat16
F32 = jnp.float32
CHIPS = 64
SB = 6
HID = 1152
HALF = 640
TOK = 128
GC = math.sqrt(2.0 / math.pi)
G1 = 2.0 * GC
G2 = 8.0 * 0.044715 * GC
CW = 384


def half_gelu(v):
    return v * jnp.tanh(v * (G1 + G2 * (v * v))) + v


def shift_chip(t, k, sign):
    out = 0
    for unit in (16, 4, 1):
        a = (t // unit) % 4
        b = (k // unit) % 4
        out = out + unit * ((a + sign * b + 4) % 4)
    return out


def main_kernel(mods, steps, wts, x0_hbm, r_out, base_out, lhs_hbm,
                gat, hst, wgt, x0, w1, w2, lh, rx, pre, act, fbuf, bas, run,
                gsem, hsem, wsem, gsend, hsend, wsend, xsem, osem, lsem, fsend, fsib, bsend, bsib, rsem, bsem):
    t = lax.axis_index('time')
    p = lax.axis_index('model')
    q = 1 - p
    blk = t * 2 + p
    row = blk // 32
    col = pl.multiple_of((blk % 32) * TOK, TOK)

    def dev(tt, pp):
        return {'time': tt, 'model': pp}

    cp_x = pltpu.make_async_copy(x0_hbm.at[row, :, pl.ds(col, TOK)], x0, xsem)
    cp_x.start()
    pltpu.make_async_copy(mods, gat.at[0, p], gsem.at[0]).start()
    pltpu.make_async_copy(steps, hst.at[0], hsem.at[0]).start()
    pltpu.make_async_copy(wts, wgt.at[p], wsem).start()
    cp_w = pltpu.make_async_remote_copy(wts, wgt.at[p], wsend, wsem, device_id=dev(t, q), device_id_type=MESH)
    cp_w.start()
    cp_g0 = pltpu.make_async_remote_copy(mods, gat.at[0, p], gsend.at[0], gsem.at[0], device_id=dev(t, q), device_id_type=MESH)
    cp_g0.start()

    def send_mods(k, carry):
        d = shift_chip(t, k, -1)
        for c in range(2):
            pltpu.make_async_remote_copy(mods, gat.at[k, p], gsend.at[k], gsem.at[k], device_id=dev(d, c), device_id_type=MESH).start()
        pltpu.make_async_remote_copy(steps, hst.at[k], hsend.at[k], hsem.at[k], device_id=dev(d, p), device_id_type=MESH).start()
        return carry

    lax.fori_loop(1, CHIPS, send_mods, 0)

    zero = jnp.zeros((16, TOK), BF)
    ones_row = jnp.where(lax.broadcasted_iota(jnp.int32, (16, TOK), 0) == 0, 1.0, 0.0).astype(BF)
    for pr in range(3):
        for r in range(8):
            for m in range(2):
                rx[pr, 16 * r:16 * r + 16, TOK * m:TOK * m + TOK] = ones_row if r == 4 * m + 3 else zero
    act[1] = jnp.zeros(act.shape[1:], BF)
    pltpu.make_async_copy(wgt, wgt, wsem).wait()
    wf = wgt[...].astype(F32)

    def merged(a, b):
        return jnp.concatenate([a[:, :512], b[:, :512], a[:, 512:] + b[:, 512:]], axis=1)

    w1[...] = merged(wf[0, :16], wf[1, :16])
    w2[...] = merged(wf[0, 16:], wf[1, 16:]).astype(BF)
    cp_x.wait()

    first = lax.broadcasted_iota(jnp.int32, (16, HID), 0) == 0

    def build(k, slot):
        mf = merged(gat[k, 0].astype(F32), gat[k, 1].astype(F32))
        w = w1[...]
        for pr in range(3):
            parts = []
            for m in range(2):
                j = 2 * pr + m
                ws = w * (0.5 * mf[j:j + 1] + 0.5)
                hi = ws.astype(BF)
                rest = ws - hi.astype(F32)
                mid = rest.astype(BF)
                low = (rest - mid.astype(F32)).astype(BF)
                bias = jnp.where(first, 0.5 * mf[SB + j:SB + j + 1], 0.0).astype(BF)
                parts += [hi, mid, low, bias]
            full = jnp.concatenate(parts, axis=0)
            for c in range(0, HID, 128):
                lh[slot, pr, c:c + 128, :] = full[:, c:c + 128].T

    def put_x(j, x):
        xb = x.astype(BF)
        pr, m = j // 2, j % 2
        for r in range(3):
            rx[pr, 64 * m + 16 * r:64 * m + 16 * r + 16, TOK * m:TOK * m + TOK] = xb

    def rx_prefix(s, c):
        for j in range(SB):
            put_x(j, s)
            s = s + fbuf[c, j]
        return s

    def body(cur, slot, finish):
        def mm1(pr, lo):
            pre[1 - cur, pr, lo:lo + CW, :] = jnp.dot(lh[slot, pr, lo:lo + CW, :], rx[pr], preferred_element_type=F32)
        rows = []
        for pr in range(3):
            acc = jnp.zeros((16, 2 * TOK), F32)
            for lo in range(0, HID, CW):
                mm1(pr, lo)
                acc = acc + jnp.dot(w2[:, lo:lo + CW], act[1 - cur, pr, lo:lo + CW, :], preferred_element_type=F32)
                act[cur, pr, lo:lo + CW, :] = half_gelu(pre[cur, pr, lo:lo + CW, :]).astype(BF)
            rows += [acc[:, :TOK], acc[:, TOK:]]
        finish(rows)

    def tail(cur, finish):
        rows = []
        for pr in range(3):
            acc = jnp.dot(w2[...], act[cur, pr], preferred_element_type=F32)
            rows += [acc[:, :TOK], acc[:, TOK:]]
        finish(rows)

    def head(slot):
        for pr in range(3):
            for lo in range(0, HID, CW):
                pre[0, pr, lo:lo + CW, :] = jnp.dot(lh[slot, pr, lo:lo + CW, :], rx[pr], preferred_element_type=F32)

    def store_f(c, kk, rows):
        tot = None
        for j in range(SB):
            f = hst[kk, j:j + 1, :] * rows[j]
            fbuf[c, j] = f
            tot = f if tot is None else tot + f
        return tot

    def wait_mods(k):
        pltpu.make_async_copy(gat.at[k], gat.at[k], gsem.at[k]).wait()
        pltpu.make_async_copy(hst.at[k], hst.at[k], hsem.at[k]).wait()

    def out_lh(k):
        return pltpu.make_async_copy(lh.at[k % 4], lhs_hbm.at[shift_chip(t, k, 1)], osem.at[k % 4])

    wait_mods(0)
    build(0, 0)
    wait_mods(1)
    build(1, 1)
    for j in range(SB):
        put_x(j, x0[...])
    head(0)
    out_lh(0).start()

    def sweep0(i, carry):
        for u in range(2):
            n = 2 * i + u

            @pl.when(n + 1 < CHIPS)
            def _():
                out_lh(n + 1).start()

            @pl.when(n + 2 < CHIPS)
            def _():
                wait_mods(n + 2)

            @pl.when((n >= 2) & (n + 2 < CHIPS))
            def _():
                out_lh(n - 2).wait()

            nb = jnp.minimum(n + 2, CHIPS - 1)
            build(nb, jnp.where(n + 2 < CHIPS, (n + 2) % 4, 4))
            prev = jnp.maximum(n - 1, 0)
            where = jnp.where(n == 0, CHIPS, shift_chip(t, prev, 1))
            body(u, jnp.where(n + 1 < CHIPS, (n + 1) % 4, 4), lambda rows: store_f(where, prev, rows))
        return carry

    lax.fori_loop(0, CHIPS // 2, sweep0, 0)
    tail(1, lambda rows: store_f(shift_chip(t, CHIPS - 1, 1), CHIPS - 1, rows))
    for k in range(CHIPS - 4, CHIPS):
        out_lh(k).wait()

    def block_of(s, n):
        if s < 3:
            return n
        return shift_chip(t, (n + 1) % CHIPS, 1)

    def in_lh(s, n, slot):
        return pltpu.make_async_copy(lhs_hbm.at[block_of(s, n)], lh.at[slot], lsem.at[slot])

    for n in range(3):
        in_lh(1, n, n).start()

    for s in (1, 2, 3):
        in_lh(s, 0, 0).wait()
        if s < 3:
            run[0] = rx_prefix(x0[...], 0)
        else:
            rx_prefix(bas[block_of(3, 0)], block_of(3, 0))
        head(0)

        def sweep(i, carry, s=s):
            for u in range(2):
                n = 2 * i + u
                slot = jnp.where(n + 1 < CHIPS, (n + 1) % 4, 4)
                nx = jnp.minimum(n + 1, CHIPS - 1)
                prev = jnp.maximum(n - 1, 0)

                @pl.when(n + 1 < CHIPS)
                def _():
                    in_lh(s, n + 1, (n + 1) % 4).wait()

                @pl.when(n + 3 < CHIPS)
                def _():
                    in_lh(s, n + 3, (n + 3) % 4).start()
                if s < 3:
                    @pl.when(n + 3 >= CHIPS)
                    def _():
                        in_lh(s + 1, n + 3 - CHIPS, (n + 3) % 4).start()
                else:
                    @pl.when(n >= 2)
                    def _():
                        send_f(n - 1)

                if s < 3:
                    run[0] = rx_prefix(run[0], nx)
                else:
                    cn = block_of(3, nx)
                    rx_prefix(bas[cn], cn)
                cp = block_of(s, prev)
                where = jnp.where(n == 0, CHIPS, cp)
                kk = shift_chip(cp, t, -1)

                def finish(rows):
                    tot = store_f(where, kk, rows)
                    if s == 2:
                        bas[where] = run[1]
                        run[1] = jnp.where(n == 0, x0[...], run[1] + tot)
                    if s == 3:
                        bas[where] = tot
                body(u, slot, finish)
            return carry

        def send_f(k):
            c = shift_chip(t, k, 1)
            for pp in range(2):
                pltpu.make_async_remote_copy(fbuf.at[c, pl.ds(0, SB - 1)], r_out.at[:, row, :, pl.ds(col, TOK)],
                                             fsend.at[k], rsem, device_id=dev(c, pp), device_id_type=MESH).start()

        lax.fori_loop(0, CHIPS // 2, sweep, 0)

        last = block_of(s, CHIPS - 1)

        def finish_last(rows, s=s, last=last):
            tot = store_f(last, shift_chip(last, t, -1) if s < 3 else 0, rows)
            if s == 2:
                bas[last] = run[1]
            if s == 3:
                bas[last] = tot
        tail(1, finish_last)

    send_f(CHIPS - 1)
    own_f = pltpu.make_async_copy(fbuf.at[t, pl.ds(0, SB - 1)], r_out.at[:, row, :, pl.ds(col, TOK)], rsem)

    def scan_base(c, s):
        tot = bas[c]
        bas[c] = s
        return s + tot

    lax.fori_loop(0, CHIPS, scan_base, x0[...])

    def send_b(k, carry):
        c = shift_chip(t, k, 1)
        for pp in range(2):
            pltpu.make_async_remote_copy(bas.at[c], base_out.at[row, :, pl.ds(col, TOK)],
                                         bsend.at[k], bsem, device_id=dev(c, pp), device_id_type=MESH).start()
        return carry

    lax.fori_loop(1, CHIPS, send_b, 0)
    own_f.start()
    sib_f = pltpu.make_async_remote_copy(fbuf.at[t, pl.ds(0, SB - 1)], r_out.at[:, row, :, pl.ds(col, TOK)],
                                         fsib, rsem, device_id=dev(t, q), device_id_type=MESH)
    sib_f.start()
    pltpu.make_async_copy(bas.at[t], base_out.at[row, :, pl.ds(col, TOK)], bsem).start()
    sib_b = pltpu.make_async_remote_copy(bas.at[t], base_out.at[row, :, pl.ds(col, TOK)],
                                         bsib, bsem, device_id=dev(t, q), device_id_type=MESH)
    sib_b.start()

    cp_w.wait_send()
    cp_g0.wait_send()

    def drain(k, carry):
        pltpu.make_async_copy(gat.at[k], gat.at[k], gsend.at[k]).wait()
        pltpu.make_async_copy(hst.at[k], hst.at[k], hsend.at[k]).wait()
        pltpu.make_async_copy(fbuf.at[pl.ds(0, 2), pl.ds(0, SB - 1)], fbuf.at[pl.ds(0, 2), pl.ds(0, SB - 1)], fsend.at[k]).wait()
        pltpu.make_async_copy(bas.at[pl.ds(0, 2)], bas.at[pl.ds(0, 2)], bsend.at[k]).wait()
        return carry

    lax.fori_loop(1, CHIPS, drain, 0)
    sib_f.wait_send()
    sib_b.wait_send()
    pltpu.make_async_copy(r_out, r_out, rsem).wait()
    pltpu.make_async_copy(base_out, base_out, bsem).wait()


def sum_kernel(r_ref, b_ref, o_ref):
    s = b_ref[...]
    o_ref[0] = s
    for j in range(SB - 1):
        s = s + r_ref[j]
        o_ref[j + 1] = s


def solution(mesh):
    def device_body(x_init, w_up, w_down, mod_scale, mod_shift, step_size):
        batch, tokens, chan = x_init.shape
        p = lax.axis_index('model')

        def spread(a):
            tail = a[:, 512:]
            z = jnp.zeros_like(tail)
            last = jnp.where(p == 0, jnp.concatenate([tail, z], axis=1), jnp.concatenate([z, tail], axis=1))
            return jnp.concatenate([a[:, :512], last], axis=1)

        mods = spread(jnp.concatenate([mod_scale, mod_shift, jnp.zeros((4, mod_scale.shape[1]), BF)], axis=0))
        wts = spread(jnp.concatenate([w_up, w_down.T], axis=0))
        steps = jnp.broadcast_to(jnp.concatenate([step_size, jnp.zeros((2,), F32)])[:, None], (8, TOK))
        x0 = jnp.swapaxes(x_init, 1, 2)
        vm = pl.BlockSpec(memory_space=pltpu.VMEM)
        hb = pl.BlockSpec(memory_space=pl.ANY)
        dma = pltpu.SemaphoreType.DMA
        r, base, _ = pl.pallas_call(
            main_kernel,
            out_shape=(
                jax.ShapeDtypeStruct((SB - 1, batch, chan, tokens), F32),
                jax.ShapeDtypeStruct((batch, chan, tokens), F32),
                jax.ShapeDtypeStruct((CHIPS, 3, HID, 128), BF),
            ),
            in_specs=[vm, vm, vm, hb],
            out_specs=(hb, hb, hb),
            scratch_shapes=[
                pltpu.VMEM((CHIPS, 2, 16, HALF), BF),
                pltpu.VMEM((CHIPS, 8, TOK), F32),
                pltpu.VMEM((2, 32, HALF), BF),
                pltpu.VMEM((chan, TOK), F32),
                pltpu.VMEM((chan, HID), F32),
                pltpu.VMEM((chan, HID), BF),
                pltpu.VMEM((5, 3, HID, 128), BF),
                pltpu.VMEM((3, 128, 2 * TOK), BF),
                pltpu.VMEM((2, 3, HID, 2 * TOK), F32),
                pltpu.VMEM((2, 3, HID, 2 * TOK), BF),
                pltpu.VMEM((CHIPS + 1, SB, chan, TOK), F32),
                pltpu.VMEM((CHIPS + 1, chan, TOK), F32),
                pltpu.VMEM((2, chan, TOK), F32),
                dma((CHIPS,)), dma((CHIPS,)), dma, dma((CHIPS,)), dma((CHIPS,)), dma, dma,
                dma((4,)), dma((4,)), dma((CHIPS,)), dma, dma((CHIPS,)), dma, dma, dma,
            ],
            compiler_params=pltpu.CompilerParams(has_side_effects=True, vmem_limit_bytes=60 * 2 ** 20),
            name='sweeps',
        )(mods, steps, wts, x0)
        tile = 1024
        out = pl.pallas_call(
            sum_kernel,
            grid=(batch, tokens // tile),
            out_shape=jax.ShapeDtypeStruct((SB, batch, chan, tokens), F32),
            in_specs=[pl.BlockSpec((SB - 1, None, chan, tile), lambda b, i: (0, b, 0, i)),
                      pl.BlockSpec((None, chan, tile), lambda b, i: (b, 0, i))],
            out_specs=pl.BlockSpec((SB, None, chan, tile), lambda b, i: (0, b, 0, i)),
            name='sums',
        )(r, base)
        return jnp.swapaxes(out, 2, 3)

    return jax.shard_map(device_body, mesh=mesh, in_specs=(P('data', None, None), P(None, 'model'), P('model', None), P('time', 'model'), P('time', 'model'), P('time')), out_specs=P('time', 'data', None, None), check_vma=False)
```

time: 1340 us -> 537 us (0.40)
  waiting for transfers between devices: 619 us -> 0 us
  Pallas kernels: 0 us -> 531 us
  matrix products: 517 us -> 0 us
  starting transfers between devices: 151 us -> 0 us
  other arithmetic: 25.4 us -> 3.63 us
  between operations: 13.8 us -> 0.02 us
    pallas_call x0 -> x2, Pallas kernels: none -> 531 us  [the longest x1 521 us: device_body(): pl.pallas_call(main_kernel, out_shape=(jax.ShapeDtypeStruct((SB - 1, batc...]
    dot_general x7 -> x0, matrix products: 517 us -> none  [the longest x3 299 us: local_drift(): jnp.einsum('tbnc,cd->tbnd', latents.astype(jnp.bfloat16), w_up, preferred...]
    ppermute x24 -> x0, waiting for transfers between devices: 459 us -> none  [device_body(): scan_acc = scan_acc + lax.ppermute(scan_acc, 'time', perm_pairs)]
    psum x4 -> x0, waiting for transfers between devices: 160 us -> none  [device_body(): drifts = step_col * lax.psum(part_drift, 'model')]
    ppermute x24 -> x0, starting transfers between devices: 151 us -> none  [device_body(): scan_acc = scan_acc + lax.ppermute(scan_acc, 'time', perm_pairs)]
    another operation x4 -> x0, other arithmetic: 15.1 us -> none  [device_body(): running = jnp.cumsum(drifts, axis=0)]
  transfers between devices with their start and end apart: 28 -> 0, of which waited for: 28 -> 0; matrix products, arithmetic and copies ran while one was open for 0% -> 0% of each run, Pallas kernels for 0% -> 0%
where the time goes in v1:
time: 537 us
  Pallas kernels  531 us (99%)
    pallas_call x1, Pallas kernels, device_body(): pl.pallas_call(main_kernel, out_shape=(jax.ShapeDtypeStruct((SB - 1, batc...  521 us
    pallas_call x1, Pallas kernels, device_body(): pl.pallas_call(sum_kernel, grid=(batch, tokens // tile), out_shape=jax.Sh...  10.8 us

profile of v1, /device:TPU:1, one launch (start us, length us, event | category | flops | bytes accessed | tf_op | source)
XLA Modules:
  0.0 536.5 jit_solution(6496865807572195484)
XLA Ops:
  0.0 0.7 concatenate.31
  0.7 0.1 pad.13.clone
  0.7 0.7 broadcast_in_dim.5.steps
  1.4 0.7 pad_maximum_fusion.2
  2.1 0.1 pad_select_fusion
  2.2 0.8 maximum_maximum_fusion
  3.0 0.1 pad_select_fusion.1
  3.1 0.6 pad_maximum_fusion.1.mods
  3.7 0.7 fusion
  4.4 0.6 pad_maximum_fusion.wts
  5.0 520.7 %sweeps.1 = (f32[5,4,16,4096]{3,2,1,0:T(8,128)}, f32[4,16,4096]{2,1,0:T(8,128)}, bf16[64,3,1152,128]{3,2,1,0:T(8,128)(2,1)}) custom-call(bf16[16,640]{1,0:T(8,128)(2,1)} %pad_maximum_fusion.1.mods, f32[8,128]{1,0:T(8,128)} %broadcast_in_dim.5.steps, bf16[32,640]{1,0:T(8,128)(2,1)} %pad_maximum_fusion.wts, f32[4,16,4096]{2,1,0:T(8,128)} %bitcast.3), custom_call_target="tpu_custom_call" | custom-call | tf_op jit(solution)/shard_map/sweeps/pallas_call | solution.py:345
  525.7 10.8 %sums.1 = f32[6,4,16,4096]{3,2,1,0:T(8,128)} custom-call(f32[5,4,16,4096]{3,2,1,0:T(8,128)} %get-tuple-element.7.r_ref, f32[4,16,4096]{2,1,0:T(8,128)} %get-tuple-element.8.b_ref), custom_call_target="tpu_custom_call" | custom-call | tf_op jit(solution)/shard_map/sums/pallas_call | solution.py:375
  (3 shorter events, 0.0 us)

commit v2 on v1

--- a/solution.py
+++ b/solution.py
@@ -20,6 +20,7 @@
 G1 = 2.0 * GC
 G2 = 8.0 * 0.044715 * GC
 CW = 384
+PAIRS = CHIPS // 2
 
 
 def half_gelu(v):
@@ -69,10 +70,11 @@
 
     zero = jnp.zeros((16, TOK), BF)
     ones_row = jnp.where(lax.broadcasted_iota(jnp.int32, (16, TOK), 0) == 0, 1.0, 0.0).astype(BF)
-    for pr in range(3):
-        for r in range(8):
-            for m in range(2):
-                rx[pr, 16 * r:16 * r + 16, TOK * m:TOK * m + TOK] = ones_row if r == 4 * m + 3 else zero
+    for b in range(2):
+        for pr in range(3):
+            for r in range(8):
+                for m in range(2):
+                    rx[b, pr, 16 * r:16 * r + 16, TOK * m:TOK * m + TOK] = ones_row if r == 4 * m + 3 else zero
     act[1] = jnp.zeros(act.shape[1:], BF)
     pltpu.make_async_copy(wgt, wgt, wsem).wait()
     wf = wgt[...].astype(F32)
@@ -86,7 +88,7 @@
 
     first = lax.broadcasted_iota(jnp.int32, (16, HID), 0) == 0
 
-    def build(k, slot):
+    def build(k, slot, half):
         mf = merged(gat[k, 0].astype(F32), gat[k, 1].astype(F32))
         w = w1[...]
         for pr in range(3):
@@ -102,28 +104,29 @@
                 parts += [hi, mid, low, bias]
             full = jnp.concatenate(parts, axis=0)
             for c in range(0, HID, 128):
-                lh[slot, pr, c:c + 128, :] = full[:, c:c + 128].T
-
-    def put_x(j, x):
+                lh[slot, half, pr, c:c + 128, :] = full[:, c:c + 128].T
+
+    def put_x(b, j, x):
         xb = x.astype(BF)
         pr, m = j // 2, j % 2
         for r in range(3):
-            rx[pr, 64 * m + 16 * r:64 * m + 16 * r + 16, TOK * m:TOK * m + TOK] = xb
-
-    def rx_prefix(s, c):
+            rx[b, pr, 64 * m + 16 * r:64 * m + 16 * r + 16, TOK * m:TOK * m + TOK] = xb
+
+    def rx_prefix(b, s, c):
         for j in range(SB):
-            put_x(j, s)
+            put_x(b, j, s)
             s = s + fbuf[c, j]
         return s
 
-    def body(cur, slot, finish):
+    def body(cur, slot, half, finish, skip=False):
         def mm1(pr, lo):
-            pre[1 - cur, pr, lo:lo + CW, :] = jnp.dot(lh[slot, pr, lo:lo + CW, :], rx[pr], preferred_element_type=F32)
+            pre[1 - cur, pr, lo:lo + CW, :] = jnp.dot(lh[slot, half, pr, lo:lo + CW, :], rx[1 - cur, pr], preferred_element_type=F32)
         rows = []
         for pr in range(3):
             acc = jnp.zeros((16, 2 * TOK), F32)
             for lo in range(0, HID, CW):
-                mm1(pr, lo)
+                if not skip:
+                    mm1(pr, lo)
                 acc = acc + jnp.dot(w2[:, lo:lo + CW], act[1 - cur, pr, lo:lo + CW, :], preferred_element_type=F32)
                 act[cur, pr, lo:lo + CW, :] = half_gelu(pre[cur, pr, lo:lo + CW, :]).astype(BF)
             rows += [acc[:, :TOK], acc[:, TOK:]]
@@ -139,7 +142,7 @@
     def head(slot):
         for pr in range(3):
             for lo in range(0, HID, CW):
-                pre[0, pr, lo:lo + CW, :] = jnp.dot(lh[slot, pr, lo:lo + CW, :], rx[pr], preferred_element_type=F32)
+                pre[0, pr, lo:lo + CW, :] = jnp.dot(lh[slot, 0, pr, lo:lo + CW, :], rx[0, pr], preferred_element_type=F32)
 
     def store_f(c, kk, rows):
         tot = None
@@ -153,93 +156,90 @@
         pltpu.make_async_copy(gat.at[k], gat.at[k], gsem.at[k]).wait()
         pltpu.make_async_copy(hst.at[k], hst.at[k], hsem.at[k]).wait()
 
-    def out_lh(k):
-        return pltpu.make_async_copy(lh.at[k % 4], lhs_hbm.at[shift_chip(t, k, 1)], osem.at[k % 4])
-
-    wait_mods(0)
-    build(0, 0)
-    wait_mods(1)
-    build(1, 1)
+    def out_lh(g, half):
+        return pltpu.make_async_copy(lh.at[g % 3, half], lhs_hbm.at[shift_chip(t, 2 * g + half, 1)], osem.at[g % 3, half])
+
+    for g in range(2):
+        for half in range(2):
+            pltpu.make_async_copy(lh.at[g + 1, half], lhs_hbm.at[CHIPS + 2 * g + half], osem.at[g + 1, half]).start()
+    for half in range(2):
+        wait_mods(half)
+        build(half, 0, half)
     for j in range(SB):
-        put_x(j, x0[...])
+        put_x(0, j, x0[...])
+        put_x(1, j, x0[...])
     head(0)
-    out_lh(0).start()
-
-    def sweep0(i, carry):
+
+    def step0(i, more):
+        for half in range(2):
+            pltpu.make_async_copy(lh.at[(i + 1) % 3, half], lhs_hbm.at[half], osem.at[(i + 1) % 3, half]).wait()
+            out_lh(i, half).start()
+            if more:
+                wait_mods(2 * i + 2 + half)
         for u in range(2):
             n = 2 * i + u
-
-            @pl.when(n + 1 < CHIPS)
-            def _():
-                out_lh(n + 1).start()
-
-            @pl.when(n + 2 < CHIPS)
-            def _():
-                wait_mods(n + 2)
-
-            @pl.when((n >= 2) & (n + 2 < CHIPS))
-            def _():
-                out_lh(n - 2).wait()
-
-            nb = jnp.minimum(n + 2, CHIPS - 1)
-            build(nb, jnp.where(n + 2 < CHIPS, (n + 2) % 4, 4))
+            if more:
+                build(n + 2, (i + 1) % 3, u)
             prev = jnp.maximum(n - 1, 0)
             where = jnp.where(n == 0, CHIPS, shift_chip(t, prev, 1))
-            body(u, jnp.where(n + 1 < CHIPS, (n + 1) % 4, 4), lambda rows: store_f(where, prev, rows))
+            body(u, (i + u) % 3, 1 - u, lambda rows: store_f(where, prev, rows), skip=(u == 1 and not more))
+
+    def loop0(i, carry):
+        step0(i, True)
         return carry
 
-    lax.fori_loop(0, CHIPS // 2, sweep0, 0)
+    lax.fori_loop(0, PAIRS - 1, loop0, 0)
+    step0(PAIRS - 1, False)
     tail(1, lambda rows: store_f(shift_chip(t, CHIPS - 1, 1), CHIPS - 1, rows))
-    for k in range(CHIPS - 4, CHIPS):
-        out_lh(k).wait()
+    for g in (PAIRS - 2, PAIRS - 1):
+        for half in range(2):
+            out_lh(g, half).wait()
 
     def block_of(s, n):
         if s < 3:
             return n
         return shift_chip(t, (n + 1) % CHIPS, 1)
 
-    def in_lh(s, n, slot):
-        return pltpu.make_async_copy(lhs_hbm.at[block_of(s, n)], lh.at[slot], lsem.at[slot])
-
-    for n in range(3):
-        in_lh(1, n, n).start()
+    def in_lh(block, g, half):
+        return pltpu.make_async_copy(lhs_hbm.at[block], lh.at[g % 3, half], lsem.at[g % 3, half])
+
+    def send_f(k):
+        c = shift_chip(t, k, 1)
+        for pp in range(2):
+            pltpu.make_async_remote_copy(fbuf.at[c, pl.ds(0, SB - 1)], r_out.at[:, row, :, pl.ds(col, TOK)],
+                                         fsend.at[k], rsem, device_id=dev(c, pp), device_id_type=MESH).start()
+
+    for g in range(2):
+        for half in range(2):
+            in_lh(2 * g + half, g, half).start()
+    for half in range(2):
+        in_lh(half, 0, half).wait()
 
     for s in (1, 2, 3):
-        in_lh(s, 0, 0).wait()
-        if s < 3:
-            run[0] = rx_prefix(x0[...], 0)
-        else:
-            rx_prefix(bas[block_of(3, 0)], block_of(3, 0))
-        head(0)
-
-        def sweep(i, carry, s=s):
+        base = PAIRS * (s - 1)
+        for b in range(2):
+            if s < 3:
+                run[0] = rx_prefix(b, run[0] if b else x0[...], b)
+            else:
+                rx_prefix(b, bas[block_of(3, b)], block_of(3, b))
+            if b == 0:
+                head(base % 3)
+
+        def step(i, send, s=s, base=base):
+            g = base + i
+            for half in range(2):
+                in_lh(0, g + 1, half).wait()
+            for half in range(2):
+                n = 2 * i + 4 + half
+                nxt = block_of(min(s + 1, 3), n % CHIPS)
+                in_lh(jnp.where(n < CHIPS, block_of(s, n % CHIPS), nxt), g + 2, half).start()
+            if send:
+                send_f(2 * i - 2)
+                send_f(2 * i - 1)
             for u in range(2):
                 n = 2 * i + u
-                slot = jnp.where(n + 1 < CHIPS, (n + 1) % 4, 4)
-                nx = jnp.minimum(n + 1, CHIPS - 1)
+                nx = jnp.minimum(n + 2, CHIPS - 1)
                 prev = jnp.maximum(n - 1, 0)
-
-                @pl.when(n + 1 < CHIPS)
-                def _():
-                    in_lh(s, n + 1, (n + 1) % 4).wait()
-
-                @pl.when(n + 3 < CHIPS)
-                def _():
-                    in_lh(s, n + 3, (n + 3) % 4).start()
-                if s < 3:
-                    @pl.when(n + 3 >= CHIPS)
-                    def _():
-                        in_lh(s + 1, n + 3 - CHIPS, (n + 3) % 4).start()
-                else:
-                    @pl.when(n >= 2)
-                    def _():
-                        send_f(n - 1)
-
-                if s < 3:
-                    run[0] = rx_prefix(run[0], nx)
-                else:
-                    cn = block_of(3, nx)
-                    rx_prefix(bas[cn], cn)
                 cp = block_of(s, prev)
                 where = jnp.where(n == 0, CHIPS, cp)
                 kk = shift_chip(cp, t, -1)
@@ -251,16 +251,27 @@
                         run[1] = jnp.where(n == 0, x0[...], run[1] + tot)
                     if s == 3:
                         bas[where] = tot
-                body(u, slot, finish)
+                body(u, (g + u) % 3, 1 - u, finish)
+                if s < 3:
+                    run[0] = rx_prefix(u, run[0], nx)
+                else:
+                    cn = block_of(3, nx)
+                    rx_prefix(u, bas[cn], cn)
+
+        def loop(i, carry, step=step):
+            step(i, False)
             return carry
 
-        def send_f(k):
-            c = shift_chip(t, k, 1)
-            for pp in range(2):
-                pltpu.make_async_remote_copy(fbuf.at[c, pl.ds(0, SB - 1)], r_out.at[:, row, :, pl.ds(col, TOK)],
-                                             fsend.at[k], rsem, device_id=dev(c, pp), device_id_type=MESH).start()
-
-        lax.fori_loop(0, CHIPS // 2, sweep, 0)
+        def loop_send(i, carry, step=step):
+            step(i, True)
+            return carry
+
+        if s < 3:
+            lax.fori_loop(0, PAIRS, loop, 0)
+        else:
+            lax.fori_loop(0, 2, loop, 0)
+            send_f(1)
+            lax.fori_loop(2, PAIRS, loop_send, 0)
 
         last = block_of(s, CHIPS - 1)
 
@@ -272,7 +283,10 @@
                 bas[last] = tot
         tail(1, finish_last)
 
+    send_f(CHIPS - 2)
     send_f(CHIPS - 1)
+    for half in range(2):
+        in_lh(0, 3 * PAIRS + 1, half).wait()
     own_f = pltpu.make_async_copy(fbuf.at[t, pl.ds(0, SB - 1)], r_out.at[:, row, :, pl.ds(col, TOK)], rsem)
 
     def scan_base(c, s):
@@ -347,7 +361,7 @@
             out_shape=(
                 jax.ShapeDtypeStruct((SB - 1, batch, chan, tokens), F32),
                 jax.ShapeDtypeStruct((batch, chan, tokens), F32),
-                jax.ShapeDtypeStruct((CHIPS, 3, HID, 128), BF),
+                jax.ShapeDtypeStruct((CHIPS + 4, 3, HID, 128), BF),
             ),
             in_specs=[vm, vm, vm, hb],
             out_specs=(hb, hb, hb),
@@ -358,15 +372,15 @@
                 pltpu.VMEM((chan, TOK), F32),
                 pltpu.VMEM((chan, HID), F32),
                 pltpu.VMEM((chan, HID), BF),
-                pltpu.VMEM((5, 3, HID, 128), BF),
-                pltpu.VMEM((3, 128, 2 * TOK), BF),
+                pltpu.VMEM((3, 2, 3, HID, 128), BF),
+                pltpu.VMEM((2, 3, 128, 2 * TOK), BF),
                 pltpu.VMEM((2, 3, HID, 2 * TOK), F32),
                 pltpu.VMEM((2, 3, HID, 2 * TOK), BF),
                 pltpu.VMEM((CHIPS + 1, SB, chan, TOK), F32),
                 pltpu.VMEM((CHIPS + 1, chan, TOK), F32),
                 pltpu.VMEM((2, chan, TOK), F32),
                 dma((CHIPS,)), dma((CHIPS,)), dma, dma((CHIPS,)), dma((CHIPS,)), dma, dma,
-                dma((4,)), dma((4,)), dma((CHIPS,)), dma, dma((CHIPS,)), dma, dma, dma,
+                dma((3, 2)), dma((3, 2)), dma((CHIPS,)), dma, dma((CHIPS,)), dma, dma, dma,
             ],
             compiler_params=pltpu.CompilerParams(has_side_effects=True, vmem_limit_bytes=60 * 2 ** 20),
             name='sweeps',

time: 537 us -> 377 us (0.70)
  Pallas kernels: 531 us -> 367 us
    pallas_call x1, Pallas kernels: 521 us -> 356 us  [device_body(): pl.pallas_call(main_kernel, out_shape=(jax.ShapeDtypeStruct((SB - 1, batc...]
where the time goes in v2:
time: 377 us; the launch traced here: 372 us
  Pallas kernels  367 us (97%)
    pallas_call x1, Pallas kernels, device_body(): pl.pallas_call(main_kernel, out_shape=(jax.ShapeDtypeStruct((SB - 1, batc...  356 us
    pallas_call x1, Pallas kernels, device_body(): pl.pallas_call(sum_kernel, grid=(batch, tokens // tile), out_shape=jax.Sh...  10.8 us

profile of v2, /device:TPU:1, one launch (start us, length us, event | category | flops | bytes accessed | tf_op | source)
XLA Modules:
  0.0 371.7 jit_solution(3438787036445843820)
XLA Ops:
  0.0 0.7 concatenate.31
  0.7 0.1 pad.13.clone
  0.7 0.7 broadcast_in_dim.5.steps
  1.4 0.7 pad_maximum_fusion.2
  2.1 0.1 pad_select_fusion
  2.2 0.8 maximum_maximum_fusion
  3.0 0.1 pad_select_fusion.1
  3.1 0.6 pad_maximum_fusion.1.mods
  3.7 0.7 fusion
  4.4 0.6 pad_maximum_fusion.wts
  5.0 355.8 %sweeps.1 = (f32[5,4,16,4096]{3,2,1,0:T(8,128)}, f32[4,16,4096]{2,1,0:T(8,128)}, bf16[68,3,1152,128]{3,2,1,0:T(8,128)(2,1)}) custom-call(bf16[16,640]{1,0:T(8,128)(2,1)} %pad_maximum_fusion.1.mods, f32[8,128]{1,0:T(8,128)} %broadcast_in_dim.5.steps, bf16[32,640]{1,0:T(8,128)(2,1)} %pad_maximum_fusion.wts, f32[4,16,4096]{2,1,0:T(8,128)} %bitcast.3), custom_call_target="tpu_custom_call" | custom-call | tf_op jit(solution)/shard_map/sweeps/pallas_call | solution.py:359
  360.9 10.8 %sums.1 = f32[6,4,16,4096]{3,2,1,0:T(8,128)} custom-call(f32[5,4,16,4096]{3,2,1,0:T(8,128)} %get-tuple-element.7.r_ref, f32[4,16,4096]{2,1,0:T(8,128)} %get-tuple-element.8.b_ref), custom_call_target="tpu_custom_call" | custom-call | tf_op jit(solution)/shard_map/sums/pallas_call | solution.py:389
  (3 shorter events, 0.0 us)

commit v3 on v2

--- a/solution.py
+++ b/solution.py
@@ -36,8 +36,8 @@
     return out
 
 
-def main_kernel(mods, steps, wts, x0_hbm, r_out, base_out, lhs_hbm,
-                gat, hst, wgt, x0, w1, w2, lh, rx, pre, act, fbuf, bas, run,
+def main_kernel(scale, shift, up, down, hs, xmax, x0_hbm, r_out, base_out, lhs_hbm, flag,
+                mods, steps, wts, gmax, gat, hst, wgt, x0, w1, w2, lh, rx, pre, act, fbuf, bas, run,
                 gsem, hsem, wsem, gsend, hsend, wsend, xsem, osem, lsem, fsend, fsib, bsend, bsib, rsem, bsem):
     t = lax.axis_index('time')
     p = lax.axis_index('model')
@@ -51,6 +51,20 @@
 
     cp_x = pltpu.make_async_copy(x0_hbm.at[row, :, pl.ds(col, TOK)], x0, xsem)
     cp_x.start()
+
+    def spread(a):
+        tail = a[:, 512:]
+        z = jnp.zeros_like(tail)
+        last = jnp.where(p == 0, jnp.concatenate([tail, z], axis=1), jnp.concatenate([z, tail], axis=1))
+        return jnp.concatenate([a[:, :512], last], axis=1)
+
+    mods[...] = spread(jnp.concatenate([scale[...].astype(F32), shift[...].astype(F32), jnp.zeros((4, scale.shape[1]), F32)], axis=0)).astype(BF)
+    for j in range(SB):
+        steps[j:j + 1, :] = jnp.full((1, TOK), hs[j], F32)
+    steps[SB:8, :] = jnp.zeros((2, TOK), F32)
+    wts[0:16, :] = spread(up[...].astype(F32)).astype(BF)
+    wts[16:32, :] = spread(down[...].astype(F32)).astype(BF)
+    gmax[...] = jnp.zeros(gmax.shape, F32)
     pltpu.make_async_copy(mods, gat.at[0, p], gsem.at[0]).start()
     pltpu.make_async_copy(steps, hst.at[0], hsem.at[0]).start()
     pltpu.make_async_copy(wts, wgt.at[p], wsem).start()
@@ -91,6 +105,7 @@
     def build(k, slot, half):
         mf = merged(gat[k, 0].astype(F32), gat[k, 1].astype(F32))
         w = w1[...]
+        gmax[...] = jnp.maximum(gmax[...], jnp.abs(mf[:12]))
         for pr in range(3):
             parts = []
             for m in range(2):
@@ -194,6 +209,25 @@
     for g in (PAIRS - 2, PAIRS - 1):
         for half in range(2):
             out_lh(g, half).wait()
+
+    def top(a):
+        return jnp.max(jnp.max(a, axis=1, keepdims=True), axis=0, keepdims=True)
+
+    wa = jnp.abs(w1[...])
+    wtop = top(wa)
+    wlow = -top(-jnp.where(wa == 0.0, 1.0, wa))
+    gtop = 1.0 + top(gmax[0:SB])
+    btop = top(gmax[SB:2 * SB])
+    dtop = top(jnp.abs(w2[...].astype(F32)))
+    habs = lax.fori_loop(0, CHIPS, lambda k, a: a + jnp.abs(hst[k]), jnp.zeros((8, TOK), F32))
+    hsum = 8.0 * top(habs)
+    xtop = jnp.full((1, 1), xmax[0], F32)
+    bound = xtop
+    for _ in range(4):
+        arg = 16.0 * bound * (1.0 + wtop) * gtop + btop
+        bound = xtop + hsum * (HID * 2.0) * dtop * arg
+    safe = (16.0 * bound * (1.0 + wtop) * gtop < 2.0 ** 100) & (wlow > 2.0 ** -80)
+    flag[...] = jnp.broadcast_to(jnp.where(safe, 1.0, 0.0), (8, TOK))
 
     def block_of(s, n):
         if s < 3:
@@ -338,34 +372,58 @@
         o_ref[j + 1] = s
 
 
+def plain(x_init, w_up, w_down, mod_scale, mod_shift, step_size):
+    time_devs = lax.axis_size('time')
+    scale_f = 1.0 + mod_scale.astype(F32)
+    shift_f = mod_shift.astype(F32)
+    step_col = step_size[:, None, None, None]
+
+    def drift(args):
+        lat, sc, sh = args
+        act = jnp.einsum('bnc,cd->bnd', lat.astype(BF), w_up, preferred_element_type=F32)
+        hidden = jax.nn.gelu(act * sc + sh, approximate=True)
+        return jnp.einsum('bnd,dc->bnc', hidden.astype(BF), w_down, preferred_element_type=F32)
+
+    def sweep(_, latents):
+        part = lax.map(drift, (latents, scale_f, shift_f))
+        drifts = step_col * (part + lax.ppermute(part, 'model', [(0, 1), (1, 0)]))
+        running = jnp.cumsum(drifts, axis=0)
+        total = running[-1]
+        acc = total
+        hop = 1
+        while hop < time_devs:
+            acc = acc + lax.ppermute(acc, 'time', [(a, a + hop) for a in range(time_devs - hop)])
+            hop = hop * 2
+        return (x_init + (acc - total))[None] + (running - drifts)
+
+    start = jnp.broadcast_to(x_init[None], (mod_scale.shape[0],) + x_init.shape)
+    return lax.fori_loop(0, 4, sweep, start)
+
+
 def solution(mesh):
     def device_body(x_init, w_up, w_down, mod_scale, mod_shift, step_size):
         batch, tokens, chan = x_init.shape
-        p = lax.axis_index('model')
-
-        def spread(a):
-            tail = a[:, 512:]
-            z = jnp.zeros_like(tail)
-            last = jnp.where(p == 0, jnp.concatenate([tail, z], axis=1), jnp.concatenate([z, tail], axis=1))
-            return jnp.concatenate([a[:, :512], last], axis=1)
-
-        mods = spread(jnp.concatenate([mod_scale, mod_shift, jnp.zeros((4, mod_scale.shape[1]), BF)], axis=0))
-        wts = spread(jnp.concatenate([w_up, w_down.T], axis=0))
-        steps = jnp.broadcast_to(jnp.concatenate([step_size, jnp.zeros((2,), F32)])[:, None], (8, TOK))
         x0 = jnp.swapaxes(x_init, 1, 2)
+        xmax = jnp.max(jnp.abs(x_init)).reshape(1)
         vm = pl.BlockSpec(memory_space=pltpu.VMEM)
+        sm = pl.BlockSpec(memory_space=pltpu.SMEM)
         hb = pl.BlockSpec(memory_space=pl.ANY)
         dma = pltpu.SemaphoreType.DMA
-        r, base, _ = pl.pallas_call(
+        r, base, _, flag = pl.pallas_call(
             main_kernel,
             out_shape=(
                 jax.ShapeDtypeStruct((SB - 1, batch, chan, tokens), F32),
                 jax.ShapeDtypeStruct((batch, chan, tokens), F32),
                 jax.ShapeDtypeStruct((CHIPS + 4, 3, HID, 128), BF),
+                jax.ShapeDtypeStruct((8, TOK), F32),
             ),
-            in_specs=[vm, vm, vm, hb],
-            out_specs=(hb, hb, hb),
+            in_specs=[vm, vm, vm, vm, sm, sm, hb],
+            out_specs=(hb, hb, hb, vm),
             scratch_shapes=[
+                pltpu.VMEM((16, HALF), BF),
+                pltpu.VMEM((8, TOK), F32),
+                pltpu.VMEM((32, HALF), BF),
+                pltpu.VMEM((2 * SB, HID), F32),
                 pltpu.VMEM((CHIPS, 2, 16, HALF), BF),
                 pltpu.VMEM((CHIPS, 8, TOK), F32),
                 pltpu.VMEM((2, 32, HALF), BF),
@@ -384,17 +442,24 @@
             ],
             compiler_params=pltpu.CompilerParams(has_side_effects=True, vmem_limit_bytes=60 * 2 ** 20),
             name='sweeps',
-        )(mods, steps, wts, x0)
-        tile = 1024
-        out = pl.pallas_call(
-            sum_kernel,
-            grid=(batch, tokens // tile),
-            out_shape=jax.ShapeDtypeStruct((SB, batch, chan, tokens), F32),
-            in_specs=[pl.BlockSpec((SB - 1, None, chan, tile), lambda b, i: (0, b, 0, i)),
-                      pl.BlockSpec((None, chan, tile), lambda b, i: (b, 0, i))],
-            out_specs=pl.BlockSpec((SB, None, chan, tile), lambda b, i: (0, b, 0, i)),
-            name='sums',
-        )(r, base)
-        return jnp.swapaxes(out, 2, 3)
+        )(mod_scale, mod_shift, w_up, w_down.T, step_size, xmax, x0)
+        tile = 2048
+
+        def fast():
+            out = pl.pallas_call(
+                sum_kernel,
+                grid=(batch, tokens // tile),
+                out_shape=jax.ShapeDtypeStruct((SB, batch, chan, tokens), F32),
+                in_specs=[pl.BlockSpec((SB - 1, None, chan, tile), lambda b, i: (0, b, 0, i)),
+                          pl.BlockSpec((None, chan, tile), lambda b, i: (b, 0, i))],
+                out_specs=pl.BlockSpec((SB, None, chan, tile), lambda b, i: (0, b, 0, i)),
+                name='sums',
+            )(r, base)
+            return jnp.swapaxes(out, 2, 3)
+
+        def slow():
+            return plain(x_init, w_up, w_down, mod_scale, mod_shift, step_size)
+
+        return lax.cond(flag[0, 0] > 0.5, fast, slow)
 
     return jax.shard_map(device_body, mesh=mesh, in_specs=(P('data', None, None), P(None, 'model'), P('model', None), P('time', 'model'), P('time', 'model'), P('time')), out_specs=P('time', 'data', None, None), check_vma=False)

time: 377 us -> 373 us (0.989)
  no operation moved by 1% of the time
where the time goes in v3:
time: 373 us; the launch traced here: 370 us
  Pallas kernels  366 us (98%)
    pallas_call x1, Pallas kernels, device_body(): pl.pallas_call(main_kernel, out_shape=(jax.ShapeDtypeStruct((SB - 1, batc...  358 us
    pallas_call x1, Pallas kernels, fast(): pl.pallas_call(sum_kernel, grid=(batch, tokens // tile), out_shape=jax.Sh...  7.73 us

profile of v3, /device:TPU:1, one launch (start us, length us, event | category | flops | bytes accessed | tf_op | source)
XLA Modules:
  0.0 369.6 jit_solution(6929356366454677329)
XLA Ops:
  0.0 1.9 abs_reduce_fusion
  1.9 358.1 %sweeps.1 = (f32[5,4,16,4096]{3,2,1,0:T(8,128)}, f32[4,16,4096]{2,1,0:T(8,128)}, bf16[68,3,1152,128]{3,2,1,0:T(8,128)(2,1)}, f32[8,128]{1,0:T(8,128)}) custom-call(bf16[6,576]{1,0:T(8,128)(2,1)} %scale.1, bf16[6,576]{1,0:T(8,128)(2,1)} %shift.1, bf16[16,576]{1,0:T(8,128)(2,1)} %up.1, bf16[16,576]{1,0:T(8,128)(2,1)} %bitcast.49, f32[6]{0:T(128)} %hs.1, ...), custom_call_target="tpu_custom_call" | custom-call | tf_op jit(solution)/shard_map/sweeps/pallas_call | solution.py:412
  360.0 1.2 slice.6
  361.8 7.8 %conditional.1 = (f32[6,4,4096,16]{2,3,1,0:T(8,128)}) conditional(s32[]{:T(128)} %bitcast.11, (f32[4,4096,16]{1,2,0:T(8,128)}, bf16[6,576]{1,0:T(8,128)(2,1)}, bf16[6,576]{1,0:T(8,128)(2,1)}, f32[6]{0:T(128)}, bf16[16,576]{1,0:T(8,128)(2,1)}, /*index=5*/bf16[576,16]{0,1:T(8,128)(2,1)}) %tuple.19, (f32[5,4,16,4096]{3,2,1,0:T(8,128)}, ...), branch_computations={%region_1.7_spmd, %region_7.8_spmd} | conditional | flops 728770688 | bytes 195864160 | solution.py:463
  361.8 7.7 %sums.1 = f32[6,4,16,4096]{3,2,1,0:T(8,128)} custom-call(f32[5,4,16,4096]{3,2,1,0:T(8,128)} %get-tuple-element.109.r_ref, f32[4,16,4096]{2,1,0:T(8,128)} %get-tuple-element.110.b_ref), custom_call_target="tpu_custom_call" | custom-call | tf_op jit(solution)/shard_map/cond/branch_1_fun/sums/pallas_call | solution.py:449

commit v4 on v3

--- a/solution.py
+++ b/solution.py
@@ -30,27 +30,28 @@
 def shift_chip(t, k, sign):
     out = 0
     for unit in (16, 4, 1):
-        a = (t // unit) % 4
-        b = (k // unit) % 4
-        out = out + unit * ((a + sign * b + 4) % 4)
+        a = lax.rem(lax.div(jnp.int32(t), jnp.int32(unit)), jnp.int32(4))
+        b = lax.rem(lax.div(jnp.int32(k), jnp.int32(unit)), jnp.int32(4))
+        out = out + unit * lax.rem(a + sign * b + 4, jnp.int32(4))
     return out
 
 
-def main_kernel(scale, shift, up, down, hs, xmax, x0_hbm, r_out, base_out, lhs_hbm, flag,
+def main_kernel(scale, shift, up, down, hs, x0_hbm, r_out, base_out, lhs_hbm, flag,
                 mods, steps, wts, gmax, gat, hst, wgt, x0, w1, w2, lh, rx, pre, act, fbuf, bas, run,
-                gsem, hsem, wsem, gsend, hsend, wsend, xsem, osem, lsem, fsend, fsib, bsend, bsib, rsem, bsem):
+                gsem, hsem, wsem, gsend, hsend, wsend, xsem, osem, lsem, fsend, psend, bsend, bsib, rsem, psem, bsem, bpsem, xall, xallsem):
     t = lax.axis_index('time')
     p = lax.axis_index('model')
     q = 1 - p
-    blk = t * 2 + p
-    row = blk // 32
-    col = pl.multiple_of((blk % 32) * TOK, TOK)
+    row = 2 * p + lax.div(t, jnp.int32(32))
+    col = pl.multiple_of(lax.rem(t, jnp.int32(32)) * TOK, TOK)
 
     def dev(tt, pp):
         return {'time': tt, 'model': pp}
 
     cp_x = pltpu.make_async_copy(x0_hbm.at[row, :, pl.ds(col, TOK)], x0, xsem)
     cp_x.start()
+    cp_all = pltpu.make_async_copy(x0_hbm, xall, xallsem)
+    cp_all.start()
 
     def spread(a):
         tail = a[:, 512:]
@@ -221,7 +222,8 @@
     dtop = top(jnp.abs(w2[...].astype(F32)))
     habs = lax.fori_loop(0, CHIPS, lambda k, a: a + jnp.abs(hst[k]), jnp.zeros((8, TOK), F32))
     hsum = 8.0 * top(habs)
-    xtop = jnp.full((1, 1), xmax[0], F32)
+    cp_all.wait()
+    xtop = top(jnp.max(jnp.abs(xall[...]), axis=0))
     bound = xtop
     for _ in range(4):
         arg = 16.0 * bound * (1.0 + wtop) * gtop + btop
@@ -232,16 +234,21 @@
     def block_of(s, n):
         if s < 3:
             return n
-        return shift_chip(t, (n + 1) % CHIPS, 1)
+        return shift_chip(t, lax.rem(jnp.int32(n + 1), jnp.int32(CHIPS)), 1)
 
     def in_lh(block, g, half):
         return pltpu.make_async_copy(lhs_hbm.at[block], lh.at[g % 3, half], lsem.at[g % 3, half])
 
     def send_f(k):
         c = shift_chip(t, k, 1)
-        for pp in range(2):
-            pltpu.make_async_remote_copy(fbuf.at[c, pl.ds(0, SB - 1)], r_out.at[:, row, :, pl.ds(col, TOK)],
-                                         fsend.at[k], rsem, device_id=dev(c, pp), device_id_type=MESH).start()
+        pltpu.make_async_remote_copy(fbuf.at[c, pl.ds(0, SB - 1)], r_out.at[:, row, :, pl.ds(col, TOK)],
+                                     fsend.at[k], rsem.at[k], device_id=dev(c, p), device_id_type=MESH).start()
+
+    def pass_on(k):
+        src = shift_chip(t, k, -1)
+        part = r_out.at[:, 2 * p + lax.div(src, jnp.int32(32)), :, pl.ds(pl.multiple_of(lax.rem(src, jnp.int32(32)) * TOK, TOK), TOK)]
+        pltpu.make_async_copy(part, part, rsem.at[k]).wait()
+        pltpu.make_async_remote_copy(part, part, psend.at[k], psem, device_id=dev(t, q), device_id_type=MESH).start()
 
     for g in range(2):
         for half in range(2):
@@ -265,11 +272,14 @@
                 in_lh(0, g + 1, half).wait()
             for half in range(2):
                 n = 2 * i + 4 + half
-                nxt = block_of(min(s + 1, 3), n % CHIPS)
-                in_lh(jnp.where(n < CHIPS, block_of(s, n % CHIPS), nxt), g + 2, half).start()
+                wrap = lax.rem(n, jnp.int32(CHIPS))
+                nxt = block_of(min(s + 1, 3), wrap)
+                in_lh(jnp.where(n < CHIPS, block_of(s, wrap), nxt), g + 2, half).start()
             if send:
                 send_f(2 * i - 2)
                 send_f(2 * i - 1)
+                pass_on(2 * i - 7)
+                pass_on(2 * i - 6)
             for u in range(2):
                 n = 2 * i + u
                 nx = jnp.minimum(n + 2, CHIPS - 1)
@@ -303,9 +313,10 @@
         if s < 3:
             lax.fori_loop(0, PAIRS, loop, 0)
         else:
-            lax.fori_loop(0, 2, loop, 0)
-            send_f(1)
-            lax.fori_loop(2, PAIRS, loop_send, 0)
+            lax.fori_loop(0, 4, loop, 0)
+            for k in range(1, 6):
+                send_f(k)
+            lax.fori_loop(4, PAIRS, loop_send, 0)
 
         last = block_of(s, CHIPS - 1)
 
@@ -321,7 +332,11 @@
     send_f(CHIPS - 1)
     for half in range(2):
         in_lh(0, 3 * PAIRS + 1, half).wait()
-    own_f = pltpu.make_async_copy(fbuf.at[t, pl.ds(0, SB - 1)], r_out.at[:, row, :, pl.ds(col, TOK)], rsem)
+    mine = r_out.at[:, row, :, pl.ds(col, TOK)]
+    own_f = pltpu.make_async_copy(fbuf.at[t, pl.ds(0, SB - 1)], mine, rsem.at[0])
+    own_f.start()
+    sib_f = pltpu.make_async_remote_copy(fbuf.at[t, pl.ds(0, SB - 1)], mine, psend.at[0], psem, device_id=dev(t, q), device_id_type=MESH)
+    sib_f.start()
 
     def scan_base(c, s):
         tot = bas[c]
@@ -332,19 +347,21 @@
 
     def send_b(k, carry):
         c = shift_chip(t, k, 1)
-        for pp in range(2):
-            pltpu.make_async_remote_copy(bas.at[c], base_out.at[row, :, pl.ds(col, TOK)],
-                                         bsend.at[k], bsem, device_id=dev(c, pp), device_id_type=MESH).start()
+        pltpu.make_async_remote_copy(bas.at[c], base_out.at[row, :, pl.ds(col, TOK)],
+                                     bsend.at[k], bsem, device_id=dev(c, p), device_id_type=MESH).start()
         return carry
 
     lax.fori_loop(1, CHIPS, send_b, 0)
-    own_f.start()
-    sib_f = pltpu.make_async_remote_copy(fbuf.at[t, pl.ds(0, SB - 1)], r_out.at[:, row, :, pl.ds(col, TOK)],
-                                         fsib, rsem, device_id=dev(t, q), device_id_type=MESH)
-    sib_f.start()
     pltpu.make_async_copy(bas.at[t], base_out.at[row, :, pl.ds(col, TOK)], bsem).start()
-    sib_b = pltpu.make_async_remote_copy(bas.at[t], base_out.at[row, :, pl.ds(col, TOK)],
-                                         bsib, bsem, device_id=dev(t, q), device_id_type=MESH)
+
+    def late(k, carry):
+        pass_on(k)
+        return carry
+
+    lax.fori_loop(CHIPS - 7, CHIPS, late, 0)
+    half_b = base_out.at[pl.ds(2 * p, 2)]
+    pltpu.make_async_copy(half_b, half_b, bsem).wait()
+    sib_b = pltpu.make_async_remote_copy(half_b, half_b, bsib, bpsem, device_id=dev(t, q), device_id_type=MESH)
     sib_b.start()
 
     cp_w.wait_send()
@@ -353,15 +370,19 @@
     def drain(k, carry):
         pltpu.make_async_copy(gat.at[k], gat.at[k], gsend.at[k]).wait()
         pltpu.make_async_copy(hst.at[k], hst.at[k], hsend.at[k]).wait()
-        pltpu.make_async_copy(fbuf.at[pl.ds(0, 2), pl.ds(0, SB - 1)], fbuf.at[pl.ds(0, 2), pl.ds(0, SB - 1)], fsend.at[k]).wait()
-        pltpu.make_async_copy(bas.at[pl.ds(0, 2)], bas.at[pl.ds(0, 2)], bsend.at[k]).wait()
+        pltpu.make_async_copy(fbuf.at[k, pl.ds(0, SB - 1)], fbuf.at[k, pl.ds(0, SB - 1)], fsend.at[k]).wait()
+        pltpu.make_async_copy(fbuf.at[k, pl.ds(0, SB - 1)], fbuf.at[k, pl.ds(0, SB - 1)], psend.at[k]).wait()
+        pltpu.make_async_copy(bas.at[k], bas.at[k], bsend.at[k]).wait()
         return carry
 
     lax.fori_loop(1, CHIPS, drain, 0)
     sib_f.wait_send()
     sib_b.wait_send()
-    pltpu.make_async_copy(r_out, r_out, rsem).wait()
-    pltpu.make_async_copy(base_out, base_out, bsem).wait()
+    own_f.wait()
+    theirs = r_out.at[:, pl.ds(2 * q, 2)]
+    pltpu.make_async_copy(theirs, theirs, psem).wait()
+    half_q = base_out.at[pl.ds(2 * q, 2)]
+    pltpu.make_async_copy(half_q, half_q, bpsem).wait()
 
 
 def sum_kernel(r_ref, b_ref, o_ref):
@@ -404,7 +425,6 @@
     def device_body(x_init, w_up, w_down, mod_scale, mod_shift, step_size):
         batch, tokens, chan = x_init.shape
         x0 = jnp.swapaxes(x_init, 1, 2)
-        xmax = jnp.max(jnp.abs(x_init)).reshape(1)
         vm = pl.BlockSpec(memory_space=pltpu.VMEM)
         sm = pl.BlockSpec(memory_space=pltpu.SMEM)
         hb = pl.BlockSpec(memory_space=pl.ANY)
@@ -417,7 +437,7 @@
                 jax.ShapeDtypeStruct((CHIPS + 4, 3, HID, 128), BF),
                 jax.ShapeDtypeStruct((8, TOK), F32),
             ),
-            in_specs=[vm, vm, vm, vm, sm, sm, hb],
+            in_specs=[vm, vm, vm, vm, sm, hb],
             out_specs=(hb, hb, hb, vm),
             scratch_shapes=[
                 pltpu.VMEM((16, HALF), BF),
@@ -438,11 +458,12 @@
                 pltpu.VMEM((CHIPS + 1, chan, TOK), F32),
                 pltpu.VMEM((2, chan, TOK), F32),
                 dma((CHIPS,)), dma((CHIPS,)), dma, dma((CHIPS,)), dma((CHIPS,)), dma, dma,
-                dma((3, 2)), dma((3, 2)), dma((CHIPS,)), dma, dma((CHIPS,)), dma, dma, dma,
+                dma((3, 2)), dma((3, 2)), dma((CHIPS,)), dma((CHIPS,)), dma((CHIPS,)), dma, dma((CHIPS,)), dma, dma, dma,
+                pltpu.VMEM((batch, chan, tokens), F32), dma,
             ],
             compiler_params=pltpu.CompilerParams(has_side_effects=True, vmem_limit_bytes=60 * 2 ** 20),
             name='sweeps',
-        )(mod_scale, mod_shift, w_up, w_down.T, step_size, xmax, x0)
+        )(mod_scale, mod_shift, w_up, w_down.T, step_size, x0)
         tile = 2048
 
         def fast():

time: 373 us -> 366 us (0.981)
  no operation moved by 1% of the time
where the time goes in v4:
time: 366 us
  Pallas kernels  364 us (99%)
    pallas_call x1, Pallas kernels, device_body(): pl.pallas_call(main_kernel, out_shape=(jax.ShapeDtypeStruct((SB - 1, batc...  356 us
    pallas_call x1, Pallas kernels, fast(): pl.pallas_call(sum_kernel, grid=(batch, tokens // tile), out_shape=jax.Sh...  7.73 us

profile of v4, /device:TPU:1, one launch (start us, length us, event | category | flops | bytes accessed | tf_op | source)
XLA Modules:
  0.0 365.8 jit_solution(14284112153338101910)
XLA Ops:
  0.0 356.2 %sweeps.1 = (f32[5,4,16,4096]{3,2,1,0:T(8,128)}, f32[4,16,4096]{2,1,0:T(8,128)}, bf16[68,3,1152,128]{3,2,1,0:T(8,128)(2,1)}, f32[8,128]{1,0:T(8,128)}) custom-call(bf16[6,576]{1,0:T(8,128)(2,1)} %scale.1, bf16[6,576]{1,0:T(8,128)(2,1)} %shift.1, bf16[16,576]{1,0:T(8,128)(2,1)} %up.1, bf16[16,576]{1,0:T(8,128)(2,1)} %bitcast.48, f32[6]{0:T(128)} %hs.1, ...), custom_call_target="tpu_custom_call" | custom-call | tf_op jit(solution)/shard_map/sweeps/pallas_call | solution.py:432
  356.2 1.2 slice.6
  358.0 7.8 %conditional.1 = (f32[6,4,4096,16]{2,3,1,0:T(8,128)}) conditional(s32[]{:T(128)} %bitcast.10, (f32[4,4096,16]{1,2,0:T(8,128)}, bf16[6,576]{1,0:T(8,128)(2,1)}, bf16[6,576]{1,0:T(8,128)(2,1)}, f32[6]{0:T(128)}, bf16[16,576]{1,0:T(8,128)(2,1)}, /*index=5*/bf16[576,16]{0,1:T(8,128)(2,1)}) %tuple.19, (f32[5,4,16,4096]{3,2,1,0:T(8,128)}, ...), branch_computations={%region_0.6_spmd, %region_6.7_spmd} | conditional | flops 728770688 | bytes 195864160 | solution.py:484
  358.1 7.7 %sums.1 = f32[6,4,16,4096]{3,2,1,0:T(8,128)} custom-call(f32[5,4,16,4096]{3,2,1,0:T(8,128)} %get-tuple-element.109.r_ref, f32[4,16,4096]{2,1,0:T(8,128)} %get-tuple-element.110.b_ref), custom_call_target="tpu_custom_call" | custom-call | tf_op jit(solution)/shard_map/cond/branch_1_fun/sums/pallas_call | solution.py:470

commit v5 on v4

--- a/solution.py
+++ b/solution.py
@@ -28,12 +28,7 @@
 
 
 def shift_chip(t, k, sign):
-    out = 0
-    for unit in (16, 4, 1):
-        a = lax.rem(lax.div(jnp.int32(t), jnp.int32(unit)), jnp.int32(4))
-        b = lax.rem(lax.div(jnp.int32(k), jnp.int32(unit)), jnp.int32(4))
-        out = out + unit * lax.rem(a + sign * b + 4, jnp.int32(4))
-    return out
+    return lax.rem(jnp.int32(t + sign * k + CHIPS), jnp.int32(CHIPS))
 
 
 def main_kernel(scale, shift, up, down, hs, x0_hbm, r_out, base_out, lhs_hbm, flag,
@@ -242,13 +237,7 @@
     def send_f(k):
         c = shift_chip(t, k, 1)
         pltpu.make_async_remote_copy(fbuf.at[c, pl.ds(0, SB - 1)], r_out.at[:, row, :, pl.ds(col, TOK)],
-                                     fsend.at[k], rsem.at[k], device_id=dev(c, p), device_id_type=MESH).start()
-
-    def pass_on(k):
-        src = shift_chip(t, k, -1)
-        part = r_out.at[:, 2 * p + lax.div(src, jnp.int32(32)), :, pl.ds(pl.multiple_of(lax.rem(src, jnp.int32(32)) * TOK, TOK), TOK)]
-        pltpu.make_async_copy(part, part, rsem.at[k]).wait()
-        pltpu.make_async_remote_copy(part, part, psend.at[k], psem, device_id=dev(t, q), device_id_type=MESH).start()
+                                     fsend.at[k], rsem, device_id=dev(c, p), device_id_type=MESH).start()
 
     for g in range(2):
         for half in range(2):
@@ -278,8 +267,6 @@
             if send:
                 send_f(2 * i - 2)
                 send_f(2 * i - 1)
-                pass_on(2 * i - 7)
-                pass_on(2 * i - 6)
             for u in range(2):
                 n = 2 * i + u
                 nx = jnp.minimum(n + 2, CHIPS - 1)
@@ -313,10 +300,9 @@
         if s < 3:
             lax.fori_loop(0, PAIRS, loop, 0)
         else:
-            lax.fori_loop(0, 4, loop, 0)
-            for k in range(1, 6):
-                send_f(k)
-            lax.fori_loop(4, PAIRS, loop_send, 0)
+            lax.fori_loop(0, 2, loop, 0)
+            send_f(1)
+            lax.fori_loop(2, PAIRS, loop_send, 0)
 
         last = block_of(s, CHIPS - 1)
 
@@ -333,10 +319,8 @@
     for half in range(2):
         in_lh(0, 3 * PAIRS + 1, half).wait()
     mine = r_out.at[:, row, :, pl.ds(col, TOK)]
-    own_f = pltpu.make_async_copy(fbuf.at[t, pl.ds(0, SB - 1)], mine, rsem.at[0])
+    own_f = pltpu.make_async_copy(fbuf.at[t, pl.ds(0, SB - 1)], mine, rsem)
     own_f.start()
-    sib_f = pltpu.make_async_remote_copy(fbuf.at[t, pl.ds(0, SB - 1)], mine, psend.at[0], psem, device_id=dev(t, q), device_id_type=MESH)
-    sib_f.start()
 
     def scan_base(c, s):
         tot = bas[c]
@@ -354,11 +338,10 @@
     lax.fori_loop(1, CHIPS, send_b, 0)
     pltpu.make_async_copy(bas.at[t], base_out.at[row, :, pl.ds(col, TOK)], bsem).start()
 
-    def late(k, carry):
-        pass_on(k)
-        return carry
-
-    lax.fori_loop(CHIPS - 7, CHIPS, late, 0)
+    half_r = r_out.at[:, pl.ds(2 * p, 2)]
+    pltpu.make_async_copy(half_r, half_r, rsem).wait()
+    sib_f = pltpu.make_async_remote_copy(half_r, half_r, psend, psem, device_id=dev(t, q), device_id_type=MESH)
+    sib_f.start()
     half_b = base_out.at[pl.ds(2 * p, 2)]
     pltpu.make_async_copy(half_b, half_b, bsem).wait()
     sib_b = pltpu.make_async_remote_copy(half_b, half_b, bsib, bpsem, device_id=dev(t, q), device_id_type=MESH)
@@ -371,14 +354,12 @@
         pltpu.make_async_copy(gat.at[k], gat.at[k], gsend.at[k]).wait()
         pltpu.make_async_copy(hst.at[k], hst.at[k], hsend.at[k]).wait()
         pltpu.make_async_copy(fbuf.at[k, pl.ds(0, SB - 1)], fbuf.at[k, pl.ds(0, SB - 1)], fsend.at[k]).wait()
-        pltpu.make_async_copy(fbuf.at[k, pl.ds(0, SB - 1)], fbuf.at[k, pl.ds(0, SB - 1)], psend.at[k]).wait()
         pltpu.make_async_copy(bas.at[k], bas.at[k], bsend.at[k]).wait()
         return carry
 
     lax.fori_loop(1, CHIPS, drain, 0)
     sib_f.wait_send()
     sib_b.wait_send()
-    own_f.wait()
     theirs = r_out.at[:, pl.ds(2 * q, 2)]
     pltpu.make_async_copy(theirs, theirs, psem).wait()
     half_q = base_out.at[pl.ds(2 * q, 2)]
@@ -458,7 +439,7 @@
                 pltpu.VMEM((CHIPS + 1, chan, TOK), F32),
                 pltpu.VMEM((2, chan, TOK), F32),
                 dma((CHIPS,)), dma((CHIPS,)), dma, dma((CHIPS,)), dma((CHIPS,)), dma, dma,
-                dma((3, 2)), dma((3, 2)), dma((CHIPS,)), dma((CHIPS,)), dma((CHIPS,)), dma, dma((CHIPS,)), dma, dma, dma,
+                dma((3, 2)), dma((3, 2)), dma((CHIPS,)), dma, dma((CHIPS,)), dma, dma, dma, dma, dma,
                 pltpu.VMEM((batch, chan, tokens), F32), dma,
             ],
             compiler_params=pltpu.CompilerParams(has_side_effects=True, vmem_limit_bytes=60 * 2 ** 20),

time: 366 us -> 345 us (0.943)
  Pallas kernels: 364 us -> 343 us
    pallas_call x1, Pallas kernels: 356 us -> 335 us  [device_body(): pl.pallas_call(main_kernel, out_shape=(jax.ShapeDtypeStruct((SB - 1, batc...]
where the time goes in v5:
time: 345 us
  Pallas kernels  343 us (99%)
    pallas_call x1, Pallas kernels, device_body(): pl.pallas_call(main_kernel, out_shape=(jax.ShapeDtypeStruct((SB - 1, batc...  335 us
    pallas_call x1, Pallas kernels, fast(): pl.pallas_call(sum_kernel, grid=(batch, tokens // tile), out_shape=jax.Sh...  7.73 us

profile of v5, /device:TPU:1, one launch (start us, length us, event | category | flops | bytes accessed | tf_op | source)
XLA Modules:
  0.0 344.6 jit_solution(7567305909757488177)
XLA Ops:
  0.0 335.0 %sweeps.1 = (f32[5,4,16,4096]{3,2,1,0:T(8,128)}, f32[4,16,4096]{2,1,0:T(8,128)}, bf16[68,3,1152,128]{3,2,1,0:T(8,128)(2,1)}, f32[8,128]{1,0:T(8,128)}) custom-call(bf16[6,576]{1,0:T(8,128)(2,1)} %scale.1, bf16[6,576]{1,0:T(8,128)(2,1)} %shift.1, bf16[16,576]{1,0:T(8,128)(2,1)} %up.1, bf16[16,576]{1,0:T(8,128)(2,1)} %bitcast.48, f32[6]{0:T(128)} %hs.1, ...), custom_call_target="tpu_custom_call" | custom-call | tf_op jit(solution)/shard_map/sweeps/pallas_call | solution.py:413
  335.0 1.2 slice.6
  336.8 7.8 %conditional.1 = (f32[6,4,4096,16]{2,3,1,0:T(8,128)}) conditional(s32[]{:T(128)} %bitcast.10, (f32[4,4096,16]{1,2,0:T(8,128)}, bf16[6,576]{1,0:T(8,128)(2,1)}, bf16[6,576]{1,0:T(8,128)(2,1)}, f32[6]{0:T(128)}, bf16[16,576]{1,0:T(8,128)(2,1)}, /*index=5*/bf16[576,16]{0,1:T(8,128)(2,1)}) %tuple.19, (f32[5,4,16,4096]{3,2,1,0:T(8,128)}, ...), branch_computations={%region_0.6_spmd, %region_6.7_spmd} | conditional | flops 728770688 | bytes 195864160 | solution.py:465
  336.8 7.7 %sums.1 = f32[6,4,16,4096]{3,2,1,0:T(8,128)} custom-call(f32[5,4,16,4096]{3,2,1,0:T(8,128)} %get-tuple-element.109.r_ref, f32[4,16,4096]{2,1,0:T(8,128)} %get-tuple-element.110.b_ref), custom_call_target="tpu_custom_call" | custom-call | tf_op jit(solution)/shard_map/cond/branch_1_fun/sums/pallas_call | solution.py:451

commit v6 on v5

--- a/solution.py
+++ b/solution.py
@@ -61,23 +61,6 @@
     wts[0:16, :] = spread(up[...].astype(F32)).astype(BF)
     wts[16:32, :] = spread(down[...].astype(F32)).astype(BF)
     gmax[...] = jnp.zeros(gmax.shape, F32)
-    pltpu.make_async_copy(mods, gat.at[0, p], gsem.at[0]).start()
-    pltpu.make_async_copy(steps, hst.at[0], hsem.at[0]).start()
-    pltpu.make_async_copy(wts, wgt.at[p], wsem).start()
-    cp_w = pltpu.make_async_remote_copy(wts, wgt.at[p], wsend, wsem, device_id=dev(t, q), device_id_type=MESH)
-    cp_w.start()
-    cp_g0 = pltpu.make_async_remote_copy(mods, gat.at[0, p], gsend.at[0], gsem.at[0], device_id=dev(t, q), device_id_type=MESH)
-    cp_g0.start()
-
-    def send_mods(k, carry):
-        d = shift_chip(t, k, -1)
-        for c in range(2):
-            pltpu.make_async_remote_copy(mods, gat.at[k, p], gsend.at[k], gsem.at[k], device_id=dev(d, c), device_id_type=MESH).start()
-        pltpu.make_async_remote_copy(steps, hst.at[k], hsend.at[k], hsem.at[k], device_id=dev(d, p), device_id_type=MESH).start()
-        return carry
-
-    lax.fori_loop(1, CHIPS, send_mods, 0)
-
     zero = jnp.zeros((16, TOK), BF)
     ones_row = jnp.where(lax.broadcasted_iota(jnp.int32, (16, TOK), 0) == 0, 1.0, 0.0).astype(BF)
     for b in range(2):
@@ -86,6 +69,23 @@
                 for m in range(2):
                     rx[b, pr, 16 * r:16 * r + 16, TOK * m:TOK * m + TOK] = ones_row if r == 4 * m + 3 else zero
     act[1] = jnp.zeros(act.shape[1:], BF)
+    pltpu.make_async_copy(mods, gat.at[0, p], gsem.at[0]).start()
+    pltpu.make_async_copy(steps, hst.at[0], hsem.at[0]).start()
+    pltpu.make_async_copy(wts, wgt.at[p], wsem).start()
+    cp_w = pltpu.make_async_remote_copy(wts, wgt.at[p], wsend, wsem, device_id=dev(t, q), device_id_type=MESH)
+    cp_w.start()
+    cp_g0 = pltpu.make_async_remote_copy(mods, gat.at[0, p], gsend.at[0], gsem.at[0], device_id=dev(t, q), device_id_type=MESH)
+    cp_g0.start()
+
+    def send_mods(k, carry):
+        d = shift_chip(t, k, -1)
+        for c in range(2):
+            pltpu.make_async_remote_copy(mods, gat.at[k, p], gsend.at[k], gsem.at[k], device_id=dev(d, c), device_id_type=MESH).start()
+        pltpu.make_async_remote_copy(steps, hst.at[k], hsend.at[k], hsem.at[k], device_id=dev(d, p), device_id_type=MESH).start()
+        return carry
+
+    lax.fori_loop(1, CHIPS, send_mods, 0)
+
     pltpu.make_async_copy(wgt, wgt, wsem).wait()
     wf = wgt[...].astype(F32)
 
@@ -445,7 +445,7 @@
             compiler_params=pltpu.CompilerParams(has_side_effects=True, vmem_limit_bytes=60 * 2 ** 20),
             name='sweeps',
         )(mod_scale, mod_shift, w_up, w_down.T, step_size, x0)
-        tile = 2048
+        tile = 4096
 
         def fast():
             out = pl.pallas_call(

time: 345 us -> 344 us (level)
  no operation moved by 1% of the time
where the time goes in v6:
time: 344 us; the launch traced here: 343 us
  Pallas kernels  341 us (99%)
    pallas_call x1, Pallas kernels, device_body(): pl.pallas_call(main_kernel, out_shape=(jax.ShapeDtypeStruct((SB - 1, batc...  335 us

profile of v6, /device:TPU:1, one launch (start us, length us, event | category | flops | bytes accessed | tf_op | source)
XLA Modules:
  0.0 342.8 jit_solution(15292814280827011845)
XLA Ops:
  0.0 335.1 %sweeps.1 = (f32[5,4,16,4096]{3,2,1,0:T(8,128)}, f32[4,16,4096]{2,1,0:T(8,128)}, bf16[68,3,1152,128]{3,2,1,0:T(8,128)(2,1)}, f32[8,128]{1,0:T(8,128)}) custom-call(bf16[6,576]{1,0:T(8,128)(2,1)} %scale.1, bf16[6,576]{1,0:T(8,128)(2,1)} %shift.1, bf16[16,576]{1,0:T(8,128)(2,1)} %up.1, bf16[16,576]{1,0:T(8,128)(2,1)} %bitcast.48, f32[6]{0:T(128)} %hs.1, ...), custom_call_target="tpu_custom_call" | custom-call | tf_op jit(solution)/shard_map/sweeps/pallas_call | solution.py:413
  335.1 1.2 slice.6
  336.9 5.9 %conditional.1 = (f32[6,4,4096,16]{2,3,1,0:T(8,128)}) conditional(s32[]{:T(128)} %bitcast.10, (f32[4,4096,16]{1,2,0:T(8,128)}, bf16[6,576]{1,0:T(8,128)(2,1)}, bf16[6,576]{1,0:T(8,128)(2,1)}, f32[6]{0:T(128)}, bf16[16,576]{1,0:T(8,128)(2,1)}, /*index=5*/bf16[576,16]{0,1:T(8,128)(2,1)}) %tuple.19, (f32[5,4,16,4096]{3,2,1,0:T(8,128)}, ...), branch_computations={%region_0.6_spmd, %region_6.7_spmd} | conditional | flops 728770688 | bytes 195864160 | solution.py:465
  337.0 5.8 %sums.1 = f32[6,4,16,4096]{3,2,1,0:T(8,128)} custom-call(f32[5,4,16,4096]{3,2,1,0:T(8,128)} %get-tuple-element.109.r_ref, f32[4,16,4096]{2,1,0:T(8,128)} %get-tuple-element.110.b_ref), custom_call_target="tpu_custom_call" | custom-call | tf_op jit(solution)/shard_map/cond/branch_1_fun/sums/pallas_call | solution.py:451
